TPU v7x, 32 devices: a whole 2x2x4 slice. The times are simulated.
32 devices in a mesh: ctx: 8 (over z, y), sub: 4 (over x, core).
Axes of the slice: x: 2, y: 2, z: 4, core: 2. Of those that a mesh axis runs over, the one named last changes fastest.
Arguments:
- queries: float32 [64, 128, 512], P('ctx', 'sub'), may hold values from -128 to 128
- keys: float32 [8, 1024, 256], P('ctx', 'sub'), may hold values from -8 to 8
- values: float32 [8, 1024, 256], P('ctx', 'sub'), may hold values from -6 to 6
- selected: int32 [64, 2, 3], P('ctx'), may hold values from 0 to 8, as said below
Outputs:
- attended: float32 [64, 128, 512], P('ctx', 'sub')
Inputs may be any that keep to these rules, and one draw needn't show every extreme that they name: `selected`: within a row the entries below the tile's own block are distinct. Within each head group, each block is named by at most one tile of each aligned run of 8 tiles. Over all head groups, each aligned run of 8 tiles names at most 1 distinct (block, group) pairs among the blocks of any one aligned run of 1 block, and some run reaches 1 in every draw. Entries that are not below the own block equal 8.
All inputs are finite; a program needn't handle non-finite values.
Results may differ from a plain program's by a relative error of at most 0.0003.
Values sent between devices are 32-bit elements; how exact they have to be, the bound alone decides.
No kernel may reach another device: no remote copies, remote signals or barrier semaphores. Data moves between devices by JAX's collectives and lax.ppermute only.
A program may use at most 64 MiB of HBM per device.

v0:
```python
import functools
import math

import jax
import jax.numpy as jnp
from jax import lax
from jax.experimental import pallas as pl
from jax.experimental.pallas import tpu as pltpu
from jax.sharding import PartitionSpec as P


QUERY_HEADS = 4
KEY_VALUE_HEADS = 2
HEAD_SIZE = 128
GROUP = QUERY_HEADS // KEY_VALUE_HEADS
CORES = 2
LANES = 128
PAD = 8

LOW_FILL = -1e30
SCALE = HEAD_SIZE ** (-0.5) * math.log2(math.e)


VMEM = pl.BlockSpec(memory_space=pltpu.VMEM)
SMEM = pl.BlockSpec(memory_space=pltpu.SMEM)
HBM = pl.BlockSpec(memory_space=pltpu.HBM)
PARAMS = pltpu.CompilerParams(vmem_limit_bytes=24 * 1024 * 1024)


def halves(x):
    high = x.astype(jnp.bfloat16)
    low = (x - high.astype(jnp.float32)).astype(jnp.bfloat16)
    return high, low


def dot_nt(a, b):
    return lax.dot_general(
        a, b, (((1,), (1,)), ((), ())), preferred_element_type=jnp.float32
    )


def dot_nn(a, b):
    return lax.dot_general(
        a, b, (((1,), (0,)), ((), ())), preferred_element_type=jnp.float32
    )


def pack_kernel(sel_hbm, q_hbm, packed_ref, route_ref, sel_ref, q_ref, sel_sem, q_sem):
    table = pltpu.make_async_copy(sel_hbm, sel_ref, sel_sem)
    table.start()
    fetch = pltpu.make_async_copy(q_hbm, q_ref, q_sem)
    fetch.start()
    tiles, rows, _ = q_ref.shape
    shards, _, _ = packed_ref.shape
    picks = sel_ref.shape[0]
    mine = lax.axis_index("ctx")
    for d in range(shards):
        route_ref[d] = -1
    table.wait()

    def visit(t, carry):
        for g in range(KEY_VALUE_HEADS):
            for c in range(picks):
                d = sel_ref[c, g, t]

                @pl.when(d < mine)
                def _():
                    route_ref[d] = t * KEY_VALUE_HEADS + g

        return carry

    lax.fori_loop(0, tiles, visit, 0)
    fetch.wait()

    def fill(d, carry):
        code = jnp.maximum(route_ref[d], 0)
        t = code // KEY_VALUE_HEADS
        g = code % KEY_VALUE_HEADS
        for h in range(GROUP):
            column = pl.multiple_of((g * GROUP + h) * HEAD_SIZE, HEAD_SIZE)
            packed_ref[d, h * rows : (h + 1) * rows, :] = q_ref[t, :, pl.ds(column, HEAD_SIZE)]
        packed_ref[d, GROUP * rows :, :] = jnp.full((PAD, LANES), g, jnp.int32).astype(jnp.float32)
        return carry

    lax.fori_loop(0, shards, fill, 0)


def source_of(sub, move, sub_count):
    step, swapped = move
    source = (sub - step * CORES + sub_count) % sub_count
    return source ^ 1 if swapped else source


def own_scores(offsets, sub_count, q_ref, k_refs, head_pair):
    tiles, rows, _ = q_ref.shape
    per_head = tiles * rows
    key_rows = k_refs[0].shape[0]
    sub = lax.axis_index("sub")
    tile_span = rows * sub_count
    q = jnp.concatenate(
        [
            q_ref[:, :, (head_pair * GROUP + h) * HEAD_SIZE : (head_pair * GROUP + h + 1) * HEAD_SIZE]
            .reshape(per_head, HEAD_SIZE)
            for h in range(GROUP)
        ],
        axis=0,
    )
    high, low = halves(q * SCALE)
    left = jnp.concatenate([high, low, high, low], axis=1)
    row = lax.broadcasted_iota(jnp.int32, (GROUP * per_head, key_rows), 0) % per_head
    row = row // rows * tile_span + row % rows + sub * rows
    column = lax.broadcasted_iota(jnp.int32, (GROUP * per_head, key_rows), 1)
    gap = column - row
    pieces = []
    for k_ref, offset in zip(k_refs, offsets):
        k_high, k_low = halves(k_ref[:, head_pair * HEAD_SIZE : (head_pair + 1) * HEAD_SIZE])
        right = jnp.concatenate([k_high, k_high, k_low, k_low], axis=1)
        score = dot_nt(left, right)
        pieces.append(jnp.where(gap <= -offset * key_rows, score, LOW_FILL))
    return pieces


def row_max(pieces):
    top = pieces[0]
    for piece in pieces[1:]:
        top = jnp.maximum(top, piece)
    return jnp.max(top, axis=1, keepdims=True)


def row_sum(pieces):
    total = pieces[0]
    for piece in pieces[1:]:
        total = total + piece
    return jnp.sum(total, axis=1, keepdims=True)


def own_values(weights, v_refs, head_pair):
    total = None
    for weight, v_ref in zip(weights, v_refs):
        w_high, w_low = halves(weight)
        v_high, v_low = halves(v_ref[:, head_pair * HEAD_SIZE : (head_pair + 1) * HEAD_SIZE])
        right = jnp.concatenate([v_high, v_low], axis=1)
        part = dot_nn(w_high, right) + dot_nn(w_low, right)
        total = part if total is None else total + part
    return total[:, :HEAD_SIZE] + total[:, HEAD_SIZE:]


def lines_of(lse, blocks, rows):
    height = lse.shape[0] // blocks
    wide = jnp.broadcast_to(lse, (lse.shape[0], LANES)).reshape(blocks, height, LANES)
    row = lax.broadcasted_iota(jnp.int32, wide.shape, 1)
    lane = lax.broadcasted_iota(jnp.int32, wide.shape, 2)
    return jnp.sum(jnp.where(row == lane - rows, wide, 0.0), axis=1)


def own_kernel(moves, sub_count, q_ref, *refs):
    count = len(moves)
    k_refs, v_refs, (base_ref, out_ref, lse_ref) = (
        refs[:count],
        refs[count : 2 * count],
        refs[2 * count :],
    )
    tiles, rows, _ = q_ref.shape
    per_head = tiles * rows
    sub = lax.axis_index("sub")
    offsets = [source_of(sub, move, sub_count) for move in moves]
    for g in range(KEY_VALUE_HEADS):
        pieces = own_scores(offsets, sub_count, q_ref, k_refs, g)
        top = row_max(pieces)
        weights = [jnp.exp2(piece - top) for piece in pieces]
        total = row_sum(weights)
        out = own_values(weights, v_refs, g) / total
        lse = top + jnp.log2(total)
        lines = None
        for h in range(GROUP):
            column = (g * GROUP + h) * HEAD_SIZE
            span = slice(h * per_head, (h + 1) * per_head)
            block = out[span].reshape(tiles, rows, HEAD_SIZE)
            base_ref[:, :, column : column + HEAD_SIZE] = block
            out_ref[:, :, column : column + HEAD_SIZE] = block
            part = lines_of(lse[span], tiles, h * rows)
            lines = part if lines is None else lines + part
        lse_ref[:, g, :] = lines


def own_pass(moves, sub_count, queries, keys, values):
    tiles = queries.shape[0]
    return pl.pallas_call(
        functools.partial(own_kernel, moves, sub_count),
        out_shape=(
            jax.ShapeDtypeStruct(queries.shape, jnp.float32),
            jax.ShapeDtypeStruct(queries.shape, jnp.float32),
            jax.ShapeDtypeStruct((tiles, KEY_VALUE_HEADS, LANES), jnp.float32),
        ),
        in_specs=[VMEM] * (1 + 2 * len(moves)),
        out_specs=(VMEM,) * 3,
        compiler_params=PARAMS,
        name="own",
    )(queries, *keys, *values)


def others(shards):
    mine = lax.axis_index("ctx")
    return [(mine + 1 + i) % shards for i in range(shards - 1)]


def pick_group(label, wide):
    picked = wide[:, :HEAD_SIZE]
    for g in range(1, KEY_VALUE_HEADS):
        picked = jnp.where(label == g, wide[:, g * HEAD_SIZE : (g + 1) * HEAD_SIZE], picked)
    return picked


def labels_of(packed_ref, slots, body):
    return jnp.concatenate(
        [jnp.broadcast_to(packed_ref[j, body : body + 1, :], (body, LANES)) for j in slots], axis=0
    )


def routed_kernel(count, packed_ref, *refs):
    k_refs, v_refs, (reply_ref, high_ref, low_ref) = (
        refs[:count],
        refs[count : 2 * count - 1],
        refs[2 * count - 1 :],
    )
    shards, span, _ = packed_ref.shape
    body = span - PAD
    slots = others(shards)
    label = labels_of(packed_ref, slots, body)
    rows = jnp.concatenate([packed_ref[j, :body, :] for j in slots], axis=0) * SCALE
    wide = jnp.concatenate(
        [jnp.where(label == g, rows, 0.0) for g in range(KEY_VALUE_HEADS)], axis=1
    )
    high, low = halves(wide)
    left = jnp.concatenate([high, low, high], axis=1)
    pieces = []
    for k_ref in k_refs:
        k_high, k_low = halves(k_ref[...])
        pieces.append(dot_nt(left, jnp.concatenate([k_high, k_high, k_low], axis=1)))
    parts = []
    for start in range(0, count, 2):
        some = pieces[start : start + 2]
        top = row_max(some)
        weights = [jnp.exp2(piece - top) for piece in some]
        total = row_sum(weights)
        result = None
        for weight, v_ref in zip(weights, v_refs[start : start + 2]):
            w_high, w_low = halves(weight)
            v_high, v_low = halves(v_ref[...])
            part = dot_nn(w_high, v_high) + dot_nn(w_low, v_high) + dot_nn(w_high, v_low)
            result = part if result is None else result + part
        parts.append((top, total, pick_group(label, result)))
    top = functools.reduce(jnp.maximum, [part[0] for part in parts])
    shrinks = [jnp.exp2(part[0] - top) for part in parts]
    total = sum(shrink * part[1] for shrink, part in zip(shrinks, parts))
    scale = 1.0 / total
    out = sum(shrink * scale * part[2] for shrink, part in zip(shrinks, parts))
    w_high, w_low = halves(weights[-1] * (shrinks[-1] * scale))
    high_ref[...] = w_high
    low_ref[...] = w_low
    lines = lines_of(top + jnp.log2(total), shards - 1, 0)
    for i, j in enumerate(slots):
        reply_ref[j, :body, :] = out[i * body : (i + 1) * body]
        reply_ref[j, body:, :] = jnp.broadcast_to(lines[i : i + 1], (PAD, LANES))


def routed_last_kernel(packed_ref, part_ref, high_ref, low_ref, v_ref, reply_ref):
    shards, span, _ = packed_ref.shape
    body = span - PAD
    slots = others(shards)
    label = labels_of(packed_ref, slots, body)
    v_high, v_low = halves(v_ref[...])
    result = (
        dot_nn(high_ref[...], v_high)
        + dot_nn(low_ref[...], v_high)
        + dot_nn(high_ref[...], v_low)
    )
    out = pick_group(label, result)
    for i, j in enumerate(slots):
        reply_ref[j, :body, :] = part_ref[j, :body, :] + out[i * body : (i + 1) * body]
        reply_ref[j, body:, :] = part_ref[j, body:, :]


def routed_pass(packed, keys, values):
    shards, span, _ = packed.shape
    count = len(keys)
    weight = jax.ShapeDtypeStruct(((shards - 1) * (span - PAD), keys[0].shape[0]), jnp.bfloat16)
    part, high, low = pl.pallas_call(
        functools.partial(routed_kernel, count),
        out_shape=(jax.ShapeDtypeStruct(packed.shape, jnp.float32), weight, weight),
        in_specs=[VMEM] * (2 * count),
        out_specs=(VMEM,) * 3,
        compiler_params=PARAMS,
        name="routed",
    )(packed, *keys, *values[:-1])
    return pl.pallas_call(
        routed_last_kernel,
        out_shape=jax.ShapeDtypeStruct(packed.shape, jnp.float32),
        in_specs=[VMEM] * 5,
        out_specs=VMEM,
        compiler_params=PARAMS,
        name="routed_last",
    )(packed, part, high, low, values[-1])


def merge_kernel(
    route_ref, reply_ref, _own, _lse, _base, own_ref, run_ref, out_ref, last_ref, sems
):
    rows = own_ref.shape[1]
    shards, span, _ = reply_ref.shape
    body = span - PAD
    width = GROUP * HEAD_SIZE

    def store(d):
        code = route_ref[d]
        t = code // KEY_VALUE_HEADS
        columns = pl.ds(pl.multiple_of(code % KEY_VALUE_HEADS * width, width), width)
        return pltpu.make_async_copy(
            own_ref.at[t, :, columns], out_ref.at[t, :, columns], sems.at[d]
        )

    def is_last(d):
        code = route_ref[d]
        return (code >= 0) & (last_ref[jnp.maximum(code, 0)] == d)

    def note(d, carry):
        code = route_ref[d]

        @pl.when(code >= 0)
        def _():
            last_ref[code] = d

        return carry

    lax.fori_loop(0, shards, note, 0)
    row = lax.broadcasted_iota(jnp.int32, (body, LANES), 0)
    lane = lax.broadcasted_iota(jnp.int32, (body, LANES), 1)

    def stand(line):
        wide = jnp.where(row == lane, jnp.broadcast_to(line, (body, LANES)), 0.0)
        return jnp.sum(wide, axis=1, keepdims=True)

    def visit(d, carry):
        code = route_ref[d]

        @pl.when(code >= 0)
        def _():
            t = code // KEY_VALUE_HEADS
            g = code % KEY_VALUE_HEADS
            ours = run_ref[t, pl.ds(g, 1), :]
            theirs = reply_ref[d, body : body + 1, :]
            top = jnp.maximum(ours, theirs)
            w_ours = jnp.exp2(ours - top)
            w_theirs = jnp.exp2(theirs - top)
            total = w_ours + w_theirs
            run_ref[t, pl.ds(g, 1), :] = top + jnp.log2(total)
            a = stand(w_ours / total)
            b = stand(w_theirs / total)
            for h in range(GROUP):
                column = pl.ds(pl.multiple_of((g * GROUP + h) * HEAD_SIZE, HEAD_SIZE), HEAD_SIZE)
                part = slice(h * rows, (h + 1) * rows)
                own_ref[t, :, column] = (
                    a[part] * own_ref[t, :, column] + b[part] * reply_ref[d, part, :]
                )

            @pl.when(last_ref[code] == d)
            def _():
                store(d).start()

        return carry

    lax.fori_loop(0, shards, visit, 0)

    def settle(d, carry):
        @pl.when(is_last(d))
        def _():
            store(d).wait()

        return carry

    lax.fori_loop(0, shards, settle, 0)


def on_device(queries, keys, values, selected):
    shards = lax.axis_size("ctx")
    sub_count = lax.axis_size("sub")
    tiles, rows, _ = queries.shape
    chips = sub_count // CORES
    span = GROUP * rows + PAD
    keys = keys.reshape(keys.shape[1:])
    values = values.reshape(values.shape[1:])

    def swap(x):
        return lax.ppermute(x, "sub", [(s, s ^ 1) for s in range(sub_count)])

    def shift(x, step):
        return lax.ppermute(
            x, "sub", [(s, (s + step * CORES) % sub_count) for s in range(sub_count)]
        )

    far_keys = [shift(keys, step) for step in range(1, chips)]
    far_values = [shift(values, step) for step in range(1, chips)]
    near_keys, near_values = [keys, swap(keys)], [values, swap(values)]

    packed, route = pl.pallas_call(
        pack_kernel,
        out_shape=(
            jax.ShapeDtypeStruct((shards, span, LANES), jnp.float32),
            jax.ShapeDtypeStruct((shards,), jnp.int32),
        ),
        in_specs=[HBM, HBM],
        out_specs=(VMEM, SMEM),
        scratch_shapes=[
            pltpu.SMEM(selected.shape[::-1], jnp.int32),
            pltpu.VMEM(queries.shape, jnp.float32),
            pltpu.SemaphoreType.DMA(()),
            pltpu.SemaphoreType.DMA(()),
        ],
        compiler_params=PARAMS,
        name="pack",
    )(
        pltpu.with_memory_space_constraint(jnp.transpose(selected, (2, 1, 0)), pltpu.HBM),
        pltpu.with_memory_space_constraint(queries, pltpu.HBM),
    )
    arrived = lax.all_to_all(packed, "ctx", split_axis=0, concat_axis=0, tiled=True)

    near_moves = ((0, False), (0, True))
    far_moves = tuple((step, swapped) for step in range(1, chips) for swapped in (False, True))
    rest_keys, rest_values = [], []
    for far_key, far_value in zip(far_keys, far_values):
        rest_keys += [far_key, swap(far_key)]
        rest_values += [far_value, swap(far_value)]
    all_keys, all_values = near_keys + rest_keys, near_values + rest_values
    reply = routed_pass(arrived, all_keys, all_values)
    answers = lax.all_to_all(reply, "ctx", split_axis=0, concat_axis=0, tiled=True)
    base, own_out, own_lse = own_pass(
        near_moves + far_moves, sub_count, queries, all_keys, all_values
    )
    return pl.pallas_call(
        merge_kernel,
        out_shape=(
            jax.ShapeDtypeStruct(own_out.shape, jnp.float32),
            jax.ShapeDtypeStruct(own_lse.shape, jnp.float32),
            jax.ShapeDtypeStruct(queries.shape, jnp.float32),
        ),
        in_specs=[SMEM, VMEM, VMEM, VMEM, HBM],
        out_specs=(VMEM, VMEM, HBM),
        input_output_aliases={2: 0, 3: 1, 4: 2},
        scratch_shapes=[
            pltpu.SMEM((tiles * KEY_VALUE_HEADS,), jnp.int32),
            pltpu.SemaphoreType.DMA((shards,)),
        ],
        compiler_params=PARAMS,
        name="merge",
    )(route, answers, own_out, own_lse, base)[2]


def solution(mesh):
    in_specs = (
        P("ctx", "sub", None),
        P("ctx", "sub", None),
        P("ctx", "sub", None),
        P("ctx", None, None),
    )
    out_specs = P("ctx", "sub", None)

    return jax.shard_map(
        on_device, mesh=mesh, in_specs=in_specs, out_specs=out_specs, check_vma=False
    )
```

profile of v0, /device:TPU:0, one launch (start us, length us, event | category | flops | bytes accessed | tf_op | source)
XLA Modules:
  0.0 36.8 jit_solution(1099791702087967522)
XLA Ops:
  0.0 3.0 %collective-permute-start.1 = (f32[256,256]{1,0:T(8,128)}, f32[256,256]{1,0:T(8,128)S(1)}, u32[]{:S(2)}, u32[]{:S(2)}) collective-permute-start(f32[256,256]{1,0:T(8,128)} %bitcast.3), channel_id=1, source_target_pairs={{0,2},{1,3},{2,0},{3,1},{4,6},{5,7},{6,4},{7,5},{8,10},{9,11},{10,... | collective-permute-start | bytes 786440 | tf_op jit(solution)/shard_map/ppermute | solution.py:397
  3.0 0.0 collective-permute-start.4
  3.0 1.9 %pack.1 = (f32[8,72,128]{2,1,0:T(8,128)}, s32[8]{0:T(128)S(1)}) custom-call(s32[3,2,8]{2,1,0:T(2,128)} %bitcast.11, f32[8,32,512]{2,1,0:T(8,128)} %q_ref.1), custom_call_target="tpu_custom_call" | custom-call | tf_op jit(solution)/shard_map/pack/pallas_call | solution.py:405
  4.9 0.0 copy-start.1
  4.9 0.0 copy-start.2
  4.9 6.5 %all-to-all-start = ((f32[8,72,128]{2,1,0:T(8,128)}), f32[8,72,128]{2,1,0:T(8,128)S(1)}, u32[]{:S(2)}, u32[]{:S(2)}) async-start(f32[8,72,128]{2,1,0:T(8,128)} %get-tuple-element.15), calls=%async_computation | async-start | bytes 589824 | tf_op jit(solution)/shard_map/all_to_all | solution.py:425
  11.4 0.0 copy-done.1
  11.4 0.1 collective-permute-start
  11.5 0.0 copy-done.2
  11.5 0.5 %collective-permute-start.3 = (f32[256,256]{1,0:T(8,128)S(1)}, f32[256,256]{1,0:T(8,128)S(1)}, u32[]{:S(2)}, u32[]{:S(2)}) collective-permute-start(f32[256,256]{1,0:T(8,128)S(1)} %bitcast.8), channel_id=1, source_target_pairs={{0,1},{1,0},{2,3},{3,2},{4,5},{5,4},{6,7},{7,6},{8,9},{9,8},{10,11... | collective-permute-start | bytes 786440 | tf_op jit(solution)/shard_map/ppermute | solution.py:394
  12.0 0.0 collective-permute-done.1.refs_2_
  12.0 0.1 collective-permute-start.2
  12.1 3.0 %collective-permute-done.4.refs_6_ = f32[256,256]{1,0:T(8,128)S(1)} collective-permute-done((f32[256,256]{1,0:T(8,128)}, f32[256,256]{1,0:T(8,128)S(1)}, u32[]{:S(2)}, u32[]{:S(2)}) %collective-permute-start.4) | collective-permute-done | bytes 262176 | tf_op jit(solution)/shard_map/ppermute | solution.py:397
  15.1 0.0 collective-permute-start.5
  15.1 0.0 collective-permute-done.refs_1_
  15.1 0.0 collective-permute-done.3.refs_5_
  15.1 5.3 %all-to-all-done.packed_ref = f32[8,72,128]{2,1,0:T(8,128)S(1)} async-done(((f32[8,72,128]{2,1,0:T(8,128)}), f32[8,72,128]{2,1,0:T(8,128)S(1)}, u32[]{:S(2)}, u32[]{:S(2)}) %all-to-all-start) | async-done | bytes 294944 | tf_op jit(solution)/shard_map/all_to_all | solution.py:425
  20.4 0.0 collective-permute-done.2.refs_3_
  20.4 1.6 %routed.1 = (f32[8,72,128]{2,1,0:T(8,128)S(1)}, bf16[448,256]{1,0:T(8,128)(2,1)S(1)}, bf16[448,256]{1,0:T(8,128)(2,1)S(1)}) custom-call(f32[8,72,128]{2,1,0:T(8,128)S(1)} %all-to-all-done.packed_ref, f32[256,256]{1,0:T(8,128)S(1)} %bitcast.5, f32[256,256]{1,0:T(8,128)S(1)} %collective-permute-done.refs_1_, f32[256,256]{1,0:T(8,128)S(1)} %collective-permute-done.1.refs_2_, ...), custom_call_target="tpu_custom_call" | custom-call | tf_op jit(solution)/shard_map/routed/pallas_call | solution.py:288
  22.0 0.0 collective-permute-done.5.v_ref.refs_7_
  22.0 1.1 %routed_last.1 = f32[8,72,128]{2,1,0:T(8,128)} custom-call(f32[8,72,128]{2,1,0:T(8,128)S(1)} %all-to-all-done.packed_ref, f32[8,72,128]{2,1,0:T(8,128)S(1)} %get-tuple-element.16.part_ref, bf16[448,256]{1,0:T(8,128)(2,1)S(1)} %get-tuple-element.17.high_ref, bf16[448,256]{1,0:T(8,128)(2,1)S(1)} %get-tuple-element.18.low_ref, ...), custom_call_target="tpu_custom_call" | custom-call | tf_op jit(solution)/shard_map/routed_last/pallas_call | solution.py:296
  23.1 0.0 copy-start
  23.1 3.8 %all-to-all-start.1 = ((f32[8,72,128]{2,1,0:T(8,128)}), f32[8,72,128]{2,1,0:T(8,128)S(1)}, u32[]{:S(2)}, u32[]{:S(2)}) async-start(f32[8,72,128]{2,1,0:T(8,128)} %routed_last.1), calls=%async_computation.1 | async-start | bytes 589824 | tf_op jit(solution)/shard_map/all_to_all | solution.py:435
  26.8 0.0 copy-done
  26.8 4.8 %own.1 = (f32[8,32,512]{2,1,0:T(8,128)}, f32[8,32,512]{2,1,0:T(8,128)S(1)}, f32[8,2,128]{2,1,0:T(2,128)S(1)}) custom-call(f32[8,32,512]{2,1,0:T(8,128)S(1)} %copy-done, f32[256,256]{1,0:T(8,128)S(1)} %bitcast.6, f32[256,256]{1,0:T(8,128)S(1)} %collective-permute-done.refs_1_, f32[256,256]{1,0:T(8,128)S(1)} %collective-permute-done.1.refs_2_, ...), custom_call_target="tpu_custom_call" | custom-call | tf_op jit(solution)/shard_map/own/pallas_call | solution.py:188
  31.7 4.2 %all-to-all-done.1.reply_ref = f32[8,72,128]{2,1,0:T(8,128)S(1)} async-done(((f32[8,72,128]{2,1,0:T(8,128)}), f32[8,72,128]{2,1,0:T(8,128)S(1)}, u32[]{:S(2)}, u32[]{:S(2)}) %all-to-all-start.1) | async-done | bytes 294944 | tf_op jit(solution)/shard_map/all_to_all | solution.py:435
  35.9 0.9 %merge.1 = (f32[8,32,512]{2,1,0:T(8,128)S(1)}, f32[8,2,128]{2,1,0:T(2,128)S(1)}, f32[8,32,512]{2,1,0:T(8,128)}) custom-call(s32[8]{0:T(128)S(1)} %get-tuple-element.14.route_ref, f32[8,72,128]{2,1,0:T(8,128)S(1)} %all-to-all-done.1.reply_ref, f32[8,32,512]{2,1,0:T(8,128)S(1)} %get-tuple-element.19._own, ...), custom_call_target="tpu_custom_call", output_to_operand_aliasing={{0}: (2, {}), {1}: (3, {}), {2}: (4, {})} | custom-call | tf_op jit(solution)/shard_map/merge/pallas_call | solution.py:439
Async XLA Ops:
  0.0 12.0 %collective-permute-start.1 = (f32[256,256]{1,0:T(8,128)}, f32[256,256]{1,0:T(8,128)S(1)}, u32[]{:S(2)}, u32[]{:S(2)}) collective-permute-start(f32[256,256]{1,0:T(8,128)} %bitcast.3), channel_id=1, source_target_pairs={{0,2},{1,3},{2,0},{3,1},{4,6},{5,7},{6,4},{7,5},{8,10},{9,11},{10,... | collective-permute-start | bytes 786440 | tf_op jit(solution)/shard_map/ppermute | solution.py:397
  3.0 12.1 %collective-permute-start.4 = (f32[256,256]{1,0:T(8,128)}, f32[256,256]{1,0:T(8,128)S(1)}, u32[]{:S(2)}, u32[]{:S(2)}) collective-permute-start(f32[256,256]{1,0:T(8,128)} %bitcast.7), channel_id=1, source_target_pairs={{0,2},{1,3},{2,0},{3,1},{4,6},{5,7},{6,4},{7,5},{8,10},{9,11},{10,... | collective-permute-start | bytes 786440 | tf_op jit(solution)/shard_map/ppermute | solution.py:397
  4.9 6.5 %copy-start.1 = (f32[1,256,256]{2,1,0:T(8,128)S(1)}, f32[1,256,256]{2,1,0:T(8,128)}, u32[]{:S(2)}) copy-start(f32[1,256,256]{2,1,0:T(8,128)} %param.5) | copy-start | bytes 786436
  4.9 6.6 %copy-start.2 = (f32[1,256,256]{2,1,0:T(8,128)S(1)}, f32[1,256,256]{2,1,0:T(8,128)}, u32[]{:S(2)}) copy-start(f32[1,256,256]{2,1,0:T(8,128)} %param.6) | copy-start | bytes 786436
  4.9 15.5 %all-to-all-start = ((f32[8,72,128]{2,1,0:T(8,128)}), f32[8,72,128]{2,1,0:T(8,128)S(1)}, u32[]{:S(2)}, u32[]{:S(2)}) async-start(f32[8,72,128]{2,1,0:T(8,128)} %get-tuple-element.15), calls=%async_computation | async-start | bytes 589824 | tf_op jit(solution)/shard_map/all_to_all | solution.py:425
  11.4 3.7 %collective-permute-start = (f32[256,256]{1,0:T(8,128)S(1)}, f32[256,256]{1,0:T(8,128)S(1)}, u32[]{:S(2)}, u32[]{:S(2)}) collective-permute-start(f32[256,256]{1,0:T(8,128)S(1)} %bitcast.4), channel_id=1, source_target_pairs={{0,1},{1,0},{2,3},{3,2},{4,5},{5,4},{6,7},{7,6},{8,9},{9,8},{10,11... | collective-permute-start | bytes 786440 | tf_op jit(solution)/shard_map/ppermute | solution.py:394
  11.5 3.6 %collective-permute-start.3 = (f32[256,256]{1,0:T(8,128)S(1)}, f32[256,256]{1,0:T(8,128)S(1)}, u32[]{:S(2)}, u32[]{:S(2)}) collective-permute-start(f32[256,256]{1,0:T(8,128)S(1)} %bitcast.8), channel_id=1, source_target_pairs={{0,1},{1,0},{2,3},{3,2},{4,5},{5,4},{6,7},{7,6},{8,9},{9,8},{10,11... | collective-permute-start | bytes 786440 | tf_op jit(solution)/shard_map/ppermute | solution.py:394
  12.0 8.4 %collective-permute-start.2 = (f32[256,256]{1,0:T(8,128)S(1)}, f32[256,256]{1,0:T(8,128)S(1)}, u32[]{:S(2)}, u32[]{:S(2)}) collective-permute-start(f32[256,256]{1,0:T(8,128)S(1)} %collective-permute-done.1.refs_2_), channel_id=1, source_target_pairs={{0,1},{1,0},{2,3},{3,2},{4,5},{5,4},{6,7},{7,6},{8,9},{9,8},{10,11... | collective-permute-start | bytes 786440 | tf_op jit(solution)/shard_map/ppermute | solution.py:394
  15.1 6.9 %collective-permute-start.5 = (f32[256,256]{1,0:T(8,128)S(1)}, f32[256,256]{1,0:T(8,128)S(1)}, u32[]{:S(2)}, u32[]{:S(2)}) collective-permute-start(f32[256,256]{1,0:T(8,128)S(1)} %collective-permute-done.4.refs_6_), channel_id=1, source_target_pairs={{0,1},{1,0},{2,3},{3,2},{4,5},{5,4},{6,7},{7,6},{8,9},{9,8},{10,11... | collective-permute-start | bytes 786440 | tf_op jit(solution)/shard_map/ppermute | solution.py:394
  23.1 3.8 %copy-start = (f32[8,32,512]{2,1,0:T(8,128)S(1)}, f32[8,32,512]{2,1,0:T(8,128)}, u32[]{:S(2)}) copy-start(f32[8,32,512]{2,1,0:T(8,128)} %q_ref.1) | copy-start | bytes 1572868
  23.1 12.8 %all-to-all-start.1 = ((f32[8,72,128]{2,1,0:T(8,128)}), f32[8,72,128]{2,1,0:T(8,128)S(1)}, u32[]{:S(2)}, u32[]{:S(2)}) async-start(f32[8,72,128]{2,1,0:T(8,128)} %routed_last.1), calls=%async_computation.1 | async-start | bytes 589824 | tf_op jit(solution)/shard_map/all_to_all | solution.py:435
where the time goes:
time: 37.2 us; the launch traced here: 36.8 us
  starting transfers between devices  13.9 us (37%)
  waiting for transfers between devices  12.6 us (34%)
  Pallas kernels  10.3 us (28%)
    all_to_all x1, starting transfers between devices, on_device(): lax.all_to_all(packed, 'ctx', split_axis=0, concat_axis=0, tiled=True)  6.49 us
    all_to_all x1, waiting for transfers between devices, on_device(): lax.all_to_all(packed, 'ctx', split_axis=0, concat_axis=0, tiled=True)  5.29 us
    pallas_call x1, Pallas kernels, own_pass(): pl.pallas_call(functools.partial(own_kernel, moves, sub_count), out_shape...  4.81 us
    all_to_all x1, waiting for transfers between devices, on_device(): lax.all_to_all(reply, 'ctx', split_axis=0, concat_axis=0, tiled=True)  4.24 us
    all_to_all x1, starting transfers between devices, on_device(): lax.all_to_all(reply, 'ctx', split_axis=0, concat_axis=0, tiled=True)  3.76 us
    ppermute x2, waiting for transfers between devices, shift(): lax.ppermute(x, 'sub', [(s, (s + step * CORES) % sub_count) for s in rang...  3.03 us
    ppermute x2, starting transfers between devices, shift(): lax.ppermute(x, 'sub', [(s, (s + step * CORES) % sub_count) for s in rang...  2.99 us
    pallas_call x1, Pallas kernels, on_device(): pl.pallas_call(pack_kernel, out_shape=(jax.ShapeDtypeStruct((shards, span...  1.88 us
  transfers between devices with their start and end apart: 8, of which 3 were waited for; matrix products, arithmetic and copies ran while one was open for 0% of the time, Pallas kernels for 22%

commit v1 on v0

--- a/solution.py
+++ b/solution.py
@@ -15,7 +15,7 @@
 GROUP = QUERY_HEADS // KEY_VALUE_HEADS
 CORES = 2
 LANES = 128
-PAD = 8
+PAD = 2
 
 LOW_FILL = -1e30
 SCALE = HEAD_SIZE ** (-0.5) * math.log2(math.e)
@@ -51,7 +51,8 @@
     fetch = pltpu.make_async_copy(q_hbm, q_ref, q_sem)
     fetch.start()
     tiles, rows, _ = q_ref.shape
-    shards, _, _ = packed_ref.shape
+    span = GROUP * rows + PAD
+    shards = packed_ref.shape[0] // span
     picks = sel_ref.shape[0]
     mine = lax.axis_index("ctx")
     for d in range(shards):
@@ -72,17 +73,16 @@
     lax.fori_loop(0, tiles, visit, 0)
     fetch.wait()
 
-    def fill(d, carry):
+    for d in range(shards):
         code = jnp.maximum(route_ref[d], 0)
         t = code // KEY_VALUE_HEADS
         g = code % KEY_VALUE_HEADS
         for h in range(GROUP):
             column = pl.multiple_of((g * GROUP + h) * HEAD_SIZE, HEAD_SIZE)
-            packed_ref[d, h * rows : (h + 1) * rows, :] = q_ref[t, :, pl.ds(column, HEAD_SIZE)]
-        packed_ref[d, GROUP * rows :, :] = jnp.full((PAD, LANES), g, jnp.int32).astype(jnp.float32)
-        return carry
-
-    lax.fori_loop(0, shards, fill, 0)
+            start = d * span + h * rows
+            packed_ref[start : start + rows, :] = q_ref[t, :, pl.ds(column, HEAD_SIZE)]
+        label = jnp.full((PAD, LANES), g, jnp.int32).astype(jnp.float32)
+        packed_ref[d * span + GROUP * rows : (d + 1) * span, :] = label
 
 
 def source_of(sub, move, sub_count):
@@ -213,21 +213,21 @@
 
 def labels_of(packed_ref, slots, body):
     return jnp.concatenate(
-        [jnp.broadcast_to(packed_ref[j, body : body + 1, :], (body, LANES)) for j in slots], axis=0
-    )
-
-
-def routed_kernel(count, packed_ref, *refs):
-    k_refs, v_refs, (reply_ref, high_ref, low_ref) = (
-        refs[:count],
-        refs[count : 2 * count - 1],
-        refs[2 * count - 1 :],
-    )
-    shards, span, _ = packed_ref.shape
+        [
+            jnp.broadcast_to(packed_ref[pl.ds(j * (body + PAD) + body, 1), :], (body, LANES))
+            for j in slots
+        ],
+        axis=0,
+    )
+
+
+def routed_kernel(count, shards, packed_ref, *refs):
+    k_refs, v_refs, reply_ref = refs[:count], refs[count : 2 * count], refs[2 * count]
+    span = packed_ref.shape[0] // shards
     body = span - PAD
     slots = others(shards)
     label = labels_of(packed_ref, slots, body)
-    rows = jnp.concatenate([packed_ref[j, :body, :] for j in slots], axis=0) * SCALE
+    rows = jnp.concatenate([packed_ref[pl.ds(j * span, body), :] for j in slots], axis=0) * SCALE
     wide = jnp.concatenate(
         [jnp.where(label == g, rows, 0.0) for g in range(KEY_VALUE_HEADS)], axis=1
     )
@@ -255,60 +255,31 @@
     total = sum(shrink * part[1] for shrink, part in zip(shrinks, parts))
     scale = 1.0 / total
     out = sum(shrink * scale * part[2] for shrink, part in zip(shrinks, parts))
-    w_high, w_low = halves(weights[-1] * (shrinks[-1] * scale))
-    high_ref[...] = w_high
-    low_ref[...] = w_low
     lines = lines_of(top + jnp.log2(total), shards - 1, 0)
     for i, j in enumerate(slots):
-        reply_ref[j, :body, :] = out[i * body : (i + 1) * body]
-        reply_ref[j, body:, :] = jnp.broadcast_to(lines[i : i + 1], (PAD, LANES))
-
-
-def routed_last_kernel(packed_ref, part_ref, high_ref, low_ref, v_ref, reply_ref):
-    shards, span, _ = packed_ref.shape
-    body = span - PAD
-    slots = others(shards)
-    label = labels_of(packed_ref, slots, body)
-    v_high, v_low = halves(v_ref[...])
-    result = (
-        dot_nn(high_ref[...], v_high)
-        + dot_nn(low_ref[...], v_high)
-        + dot_nn(high_ref[...], v_low)
-    )
-    out = pick_group(label, result)
-    for i, j in enumerate(slots):
-        reply_ref[j, :body, :] = part_ref[j, :body, :] + out[i * body : (i + 1) * body]
-        reply_ref[j, body:, :] = part_ref[j, body:, :]
-
-
-def routed_pass(packed, keys, values):
-    shards, span, _ = packed.shape
+        reply_ref[pl.ds(j * span, body), :] = out[i * body : (i + 1) * body]
+        reply_ref[pl.ds(j * span + body, PAD), :] = jnp.broadcast_to(lines[i : i + 1], (PAD, LANES))
+
+
+def routed_pass(shards, packed, keys, values):
     count = len(keys)
-    weight = jax.ShapeDtypeStruct(((shards - 1) * (span - PAD), keys[0].shape[0]), jnp.bfloat16)
-    part, high, low = pl.pallas_call(
-        functools.partial(routed_kernel, count),
-        out_shape=(jax.ShapeDtypeStruct(packed.shape, jnp.float32), weight, weight),
-        in_specs=[VMEM] * (2 * count),
-        out_specs=(VMEM,) * 3,
+    return pl.pallas_call(
+        functools.partial(routed_kernel, count, shards),
+        out_shape=jax.ShapeDtypeStruct(packed.shape, jnp.float32),
+        in_specs=[VMEM] * (1 + 2 * count),
+        out_specs=VMEM,
         compiler_params=PARAMS,
         name="routed",
-    )(packed, *keys, *values[:-1])
-    return pl.pallas_call(
-        routed_last_kernel,
-        out_shape=jax.ShapeDtypeStruct(packed.shape, jnp.float32),
-        in_specs=[VMEM] * 5,
-        out_specs=VMEM,
-        compiler_params=PARAMS,
-        name="routed_last",
-    )(packed, part, high, low, values[-1])
+    )(packed, *keys, *values)
 
 
 def merge_kernel(
     route_ref, reply_ref, _own, _lse, _base, own_ref, run_ref, out_ref, last_ref, sems
 ):
     rows = own_ref.shape[1]
-    shards, span, _ = reply_ref.shape
-    body = span - PAD
+    body = GROUP * rows
+    span = body + PAD
+    shards = reply_ref.shape[0] // span
     width = GROUP * HEAD_SIZE
 
     def store(d):
@@ -348,7 +319,7 @@
             t = code // KEY_VALUE_HEADS
             g = code % KEY_VALUE_HEADS
             ours = run_ref[t, pl.ds(g, 1), :]
-            theirs = reply_ref[d, body : body + 1, :]
+            theirs = reply_ref[pl.ds(d * span + body, 1), :]
             top = jnp.maximum(ours, theirs)
             w_ours = jnp.exp2(ours - top)
             w_theirs = jnp.exp2(theirs - top)
@@ -360,7 +331,8 @@
                 column = pl.ds(pl.multiple_of((g * GROUP + h) * HEAD_SIZE, HEAD_SIZE), HEAD_SIZE)
                 part = slice(h * rows, (h + 1) * rows)
                 own_ref[t, :, column] = (
-                    a[part] * own_ref[t, :, column] + b[part] * reply_ref[d, part, :]
+                    a[part] * own_ref[t, :, column]
+                    + b[part] * reply_ref[pl.ds(d * span + h * rows, rows), :]
                 )
 
             @pl.when(last_ref[code] == d)
@@ -390,6 +362,11 @@
     keys = keys.reshape(keys.shape[1:])
     values = values.reshape(values.shape[1:])
 
+    def exchange(x):
+        parted = x.reshape(shards, span // PAD, PAD, LANES)
+        moved = lax.all_to_all(parted, "ctx", split_axis=0, concat_axis=0, tiled=True)
+        return moved.reshape(x.shape)
+
     def swap(x):
         return lax.ppermute(x, "sub", [(s, s ^ 1) for s in range(sub_count)])
 
@@ -405,7 +382,7 @@
     packed, route = pl.pallas_call(
         pack_kernel,
         out_shape=(
-            jax.ShapeDtypeStruct((shards, span, LANES), jnp.float32),
+            jax.ShapeDtypeStruct((shards * span, LANES), jnp.float32),
             jax.ShapeDtypeStruct((shards,), jnp.int32),
         ),
         in_specs=[HBM, HBM],
@@ -422,7 +399,7 @@
         pltpu.with_memory_space_constraint(jnp.transpose(selected, (2, 1, 0)), pltpu.HBM),
         pltpu.with_memory_space_constraint(queries, pltpu.HBM),
     )
-    arrived = lax.all_to_all(packed, "ctx", split_axis=0, concat_axis=0, tiled=True)
+    arrived = exchange(packed)
 
     near_moves = ((0, False), (0, True))
     far_moves = tuple((step, swapped) for step in range(1, chips) for swapped in (False, True))
@@ -431,8 +408,8 @@
         rest_keys += [far_key, swap(far_key)]
         rest_values += [far_value, swap(far_value)]
     all_keys, all_values = near_keys + rest_keys, near_values + rest_values
-    reply = routed_pass(arrived, all_keys, all_values)
-    answers = lax.all_to_all(reply, "ctx", split_axis=0, concat_axis=0, tiled=True)
+    reply = routed_pass(shards, arrived, all_keys, all_values)
+    answers = exchange(reply)
     base, own_out, own_lse = own_pass(
         near_moves + far_moves, sub_count, queries, all_keys, all_values
     )

time: 37.2 us -> 36.1 us (0.970)
  waiting for transfers between devices: 12.6 us -> 11.8 us
    all_to_all x2, waiting for transfers between devices: 9.54 us -> 8.66 us  [exchange(): lax.all_to_all(parted, 'ctx', split_axis=0, concat_axis=0, tiled=True)]
    pallas_call x3 -> x2, Pallas kernels: 4.52 us -> 4.43 us  [the longest x1 2.62 us: routed_pass(): pl.pallas_call(functools.partial(routed_kernel, count, shards), out_shape...]
  transfers between devices with their start and end apart: 8 -> 8, of which waited for: 3 -> 3; matrix products, arithmetic and copies ran while one was open for 0% -> 0% of each run, Pallas kernels for 22% -> 19%
where the time goes in v1:
time: 36.1 us; the launch traced here: 35.8 us
  starting transfers between devices  13.7 us (38%)
  waiting for transfers between devices  11.8 us (33%)
  Pallas kernels  10.2 us (28%)
    all_to_all x2, starting transfers between devices, exchange(): lax.all_to_all(parted, 'ctx', split_axis=0, concat_axis=0, tiled=True)  10.1 us
    all_to_all x2, waiting for transfers between devices, exchange(): lax.all_to_all(parted, 'ctx', split_axis=0, concat_axis=0, tiled=True)  8.66 us
    pallas_call x1, Pallas kernels, own_pass(): pl.pallas_call(functools.partial(own_kernel, moves, sub_count), out_shape...  4.85 us
    ppermute x2, waiting for transfers between devices, shift(): lax.ppermute(x, 'sub', [(s, (s + step * CORES) % sub_count) for s in rang...  3.1 us
    ppermute x2, starting transfers between devices, shift(): lax.ppermute(x, 'sub', [(s, (s + step * CORES) % sub_count) for s in rang...  2.99 us
    pallas_call x1, Pallas kernels, routed_pass(): pl.pallas_call(functools.partial(routed_kernel, count, shards), out_shape...  2.62 us
    pallas_call x1, Pallas kernels, on_device(): pl.pallas_call(pack_kernel, out_shape=(jax.ShapeDtypeStruct((shards * spa...  1.81 us
    pallas_call x1, Pallas kernels, on_device(): pl.pallas_call(merge_kernel, out_shape=(jax.ShapeDtypeStruct(own_out.shap...  0.92 us
  transfers between devices with their start and end apart: 8, of which 3 were waited for; matrix products, arithmetic and copies ran while one was open for 0% of the time, Pallas kernels for 19%

profile of v1, /device:TPU:0, one launch (start us, length us, event | category | flops | bytes accessed | tf_op | source)
XLA Modules:
  0.0 35.8 jit_solution(4453945497550497149)
XLA Ops:
  0.0 3.0 %collective-permute-start.1 = (f32[256,256]{1,0:T(8,128)}, f32[256,256]{1,0:T(8,128)S(1)}, u32[]{:S(2)}, u32[]{:S(2)}) collective-permute-start(f32[256,256]{1,0:T(8,128)} %bitcast.9), channel_id=1, source_target_pairs={{0,2},{1,3},{2,0},{3,1},{4,6},{5,7},{6,4},{7,5},{8,10},{9,11},{10,... | collective-permute-start | bytes 786440 | tf_op jit(solution)/shard_map/ppermute | solution.py:374
  3.0 0.0 collective-permute-start.4
  3.0 1.8 %pack.1 = (f32[528,128]{1,0:T(8,128)}, s32[8]{0:T(128)S(1)}) custom-call(s32[3,2,8]{2,1,0:T(2,128)} %bitcast.17, f32[8,32,512]{2,1,0:T(8,128)} %q_ref.1), custom_call_target="tpu_custom_call" | custom-call | tf_op jit(solution)/shard_map/pack/pallas_call | solution.py:382
  4.8 0.0 copy-start.1
  4.8 0.0 copy-start.2
  4.8 6.5 %all-to-all-start = ((f32[8,33,2,128]{3,2,1,0:T(2,128)}), f32[8,33,2,128]{3,2,1,0:T(2,128)S(1)}, u32[]{:S(2)}, u32[]{:S(2)}) async-start(f32[8,33,2,128]{3,2,1,0:T(2,128)} %bitcast.1), calls=%async_computation | async-start | bytes 540672 | tf_op jit(solution)/shard_map/all_to_all | solution.py:367
  11.3 0.0 copy-done.1
  11.3 0.1 collective-permute-start
  11.4 0.0 copy-done.2
  11.4 0.5 %collective-permute-start.3 = (f32[256,256]{1,0:T(8,128)S(1)}, f32[256,256]{1,0:T(8,128)S(1)}, u32[]{:S(2)}, u32[]{:S(2)}) collective-permute-start(f32[256,256]{1,0:T(8,128)S(1)} %bitcast.14), channel_id=1, source_target_pairs={{0,1},{1,0},{2,3},{3,2},{4,5},{5,4},{6,7},{7,6},{8,9},{9,8},{10,11... | collective-permute-start | bytes 786440 | tf_op jit(solution)/shard_map/ppermute | solution.py:371
  11.9 0.0 collective-permute-done.1.refs_2_
  11.9 0.1 collective-permute-start.2
  12.0 3.1 %collective-permute-done.4.refs_6_ = f32[256,256]{1,0:T(8,128)S(1)} collective-permute-done((f32[256,256]{1,0:T(8,128)}, f32[256,256]{1,0:T(8,128)S(1)}, u32[]{:S(2)}, u32[]{:S(2)}) %collective-permute-start.4) | collective-permute-done | bytes 262176 | tf_op jit(solution)/shard_map/ppermute | solution.py:374
  15.1 0.0 collective-permute-start.5
  15.1 0.0 collective-permute-done.refs_1_
  15.1 0.0 collective-permute-done.3.refs_5_
  15.1 4.9 %all-to-all-done = f32[8,33,2,128]{3,2,1,0:T(2,128)S(1)} async-done(((f32[8,33,2,128]{3,2,1,0:T(2,128)}), f32[8,33,2,128]{3,2,1,0:T(2,128)S(1)}, u32[]{:S(2)}, u32[]{:S(2)}) %all-to-all-start) | async-done | bytes 270368 | tf_op jit(solution)/shard_map/all_to_all | solution.py:367
  20.0 0.0 collective-permute-done.2.refs_3_
  20.0 0.0 collective-permute-done.5.refs_7_
  20.0 2.6 %routed.1 = f32[528,128]{1,0:T(8,128)} custom-call(f32[528,128]{1,0:T(8,128)S(1)} %bitcast.7, f32[256,256]{1,0:T(8,128)S(1)} %bitcast.11, f32[256,256]{1,0:T(8,128)S(1)} %collective-permute-done.refs_1_, f32[256,256]{1,0:T(8,128)S(1)} %collective-permute-done.1.refs_2_, f32[256,256]{1,0:T(8,128)S(1)} %collective-permute-done.2.refs_3_, ...), custom_call_target="tpu_custom_call" | custom-call | tf_op jit(solution)/shard_map/routed/pallas_call | solution.py:266
  22.6 0.0 copy-start
  22.6 3.6 %all-to-all-start.1 = ((f32[8,33,2,128]{3,2,1,0:T(2,128)}), f32[8,33,2,128]{3,2,1,0:T(2,128)S(1)}, u32[]{:S(2)}, u32[]{:S(2)}) async-start(f32[8,33,2,128]{3,2,1,0:T(2,128)} %bitcast.5), calls=%async_computation.1 | async-start | bytes 540672 | tf_op jit(solution)/shard_map/all_to_all | solution.py:367
  26.2 0.0 copy-done
  26.2 4.8 %own.1 = (f32[8,32,512]{2,1,0:T(8,128)}, f32[8,32,512]{2,1,0:T(8,128)S(1)}, f32[8,2,128]{2,1,0:T(2,128)S(1)}) custom-call(f32[8,32,512]{2,1,0:T(8,128)S(1)} %copy-done, f32[256,256]{1,0:T(8,128)S(1)} %bitcast.12, f32[256,256]{1,0:T(8,128)S(1)} %collective-permute-done.refs_1_, f32[256,256]{1,0:T(8,128)S(1)} %collective-permute-done.1.refs_2_, ...), custom_call_target="tpu_custom_call" | custom-call | tf_op jit(solution)/shard_map/own/pallas_call | solution.py:188
  31.1 3.8 %all-to-all-done.1 = f32[8,33,2,128]{3,2,1,0:T(2,128)S(1)} async-done(((f32[8,33,2,128]{3,2,1,0:T(2,128)}), f32[8,33,2,128]{3,2,1,0:T(2,128)S(1)}, u32[]{:S(2)}, u32[]{:S(2)}) %all-to-all-start.1) | async-done | bytes 270368 | tf_op jit(solution)/shard_map/all_to_all | solution.py:367
  34.9 0.9 %merge.1 = (f32[8,32,512]{2,1,0:T(8,128)S(1)}, f32[8,2,128]{2,1,0:T(2,128)S(1)}, f32[8,32,512]{2,1,0:T(8,128)}) custom-call(s32[8]{0:T(128)S(1)} %get-tuple-element.11.route_ref, f32[528,128]{1,0:T(8,128)S(1)} %bitcast.8, f32[8,32,512]{2,1,0:T(8,128)S(1)} %get-tuple-element.13._own, ...), custom_call_target="tpu_custom_call", output_to_operand_aliasing={{0}: (2, {}), {1}: (3, {}), {2}: (4, {})} | custom-call | tf_op jit(solution)/shard_map/merge/pallas_call | solution.py:416
Async XLA Ops:
  0.0 11.9 %collective-permute-start.1 = (f32[256,256]{1,0:T(8,128)}, f32[256,256]{1,0:T(8,128)S(1)}, u32[]{:S(2)}, u32[]{:S(2)}) collective-permute-start(f32[256,256]{1,0:T(8,128)} %bitcast.9), channel_id=1, source_target_pairs={{0,2},{1,3},{2,0},{3,1},{4,6},{5,7},{6,4},{7,5},{8,10},{9,11},{10,... | collective-permute-start | bytes 786440 | tf_op jit(solution)/shard_map/ppermute | solution.py:374
  3.0 12.1 %collective-permute-start.4 = (f32[256,256]{1,0:T(8,128)}, f32[256,256]{1,0:T(8,128)S(1)}, u32[]{:S(2)}, u32[]{:S(2)}) collective-permute-start(f32[256,256]{1,0:T(8,128)} %bitcast.13), channel_id=1, source_target_pairs={{0,2},{1,3},{2,0},{3,1},{4,6},{5,7},{6,4},{7,5},{8,10},{9,11},{10,... | collective-permute-start | bytes 786440 | tf_op jit(solution)/shard_map/ppermute | solution.py:374
  4.8 6.5 %copy-start.1 = (f32[1,256,256]{2,1,0:T(8,128)S(1)}, f32[1,256,256]{2,1,0:T(8,128)}, u32[]{:S(2)}) copy-start(f32[1,256,256]{2,1,0:T(8,128)} %param.5) | copy-start | bytes 786436
  4.8 6.6 %copy-start.2 = (f32[1,256,256]{2,1,0:T(8,128)S(1)}, f32[1,256,256]{2,1,0:T(8,128)}, u32[]{:S(2)}) copy-start(f32[1,256,256]{2,1,0:T(8,128)} %param.6) | copy-start | bytes 786436
  4.8 15.1 %all-to-all-start = ((f32[8,33,2,128]{3,2,1,0:T(2,128)}), f32[8,33,2,128]{3,2,1,0:T(2,128)S(1)}, u32[]{:S(2)}, u32[]{:S(2)}) async-start(f32[8,33,2,128]{3,2,1,0:T(2,128)} %bitcast.1), calls=%async_computation | async-start | bytes 540672 | tf_op jit(solution)/shard_map/all_to_all | solution.py:367
  11.3 3.8 %collective-permute-start = (f32[256,256]{1,0:T(8,128)S(1)}, f32[256,256]{1,0:T(8,128)S(1)}, u32[]{:S(2)}, u32[]{:S(2)}) collective-permute-start(f32[256,256]{1,0:T(8,128)S(1)} %bitcast.10), channel_id=1, source_target_pairs={{0,1},{1,0},{2,3},{3,2},{4,5},{5,4},{6,7},{7,6},{8,9},{9,8},{10,11... | collective-permute-start | bytes 786440 | tf_op jit(solution)/shard_map/ppermute | solution.py:371
  11.4 3.7 %collective-permute-start.3 = (f32[256,256]{1,0:T(8,128)S(1)}, f32[256,256]{1,0:T(8,128)S(1)}, u32[]{:S(2)}, u32[]{:S(2)}) collective-permute-start(f32[256,256]{1,0:T(8,128)S(1)} %bitcast.14), channel_id=1, source_target_pairs={{0,1},{1,0},{2,3},{3,2},{4,5},{5,4},{6,7},{7,6},{8,9},{9,8},{10,11... | collective-permute-start | bytes 786440 | tf_op jit(solution)/shard_map/ppermute | solution.py:371
  11.9 8.1 %collective-permute-start.2 = (f32[256,256]{1,0:T(8,128)S(1)}, f32[256,256]{1,0:T(8,128)S(1)}, u32[]{:S(2)}, u32[]{:S(2)}) collective-permute-start(f32[256,256]{1,0:T(8,128)S(1)} %collective-permute-done.1.refs_2_), channel_id=1, source_target_pairs={{0,1},{1,0},{2,3},{3,2},{4,5},{5,4},{6,7},{7,6},{8,9},{9,8},{10,11... | collective-permute-start | bytes 786440 | tf_op jit(solution)/shard_map/ppermute | solution.py:371
  15.1 4.9 %collective-permute-start.5 = (f32[256,256]{1,0:T(8,128)S(1)}, f32[256,256]{1,0:T(8,128)S(1)}, u32[]{:S(2)}, u32[]{:S(2)}) collective-permute-start(f32[256,256]{1,0:T(8,128)S(1)} %collective-permute-done.4.refs_6_), channel_id=1, source_target_pairs={{0,1},{1,0},{2,3},{3,2},{4,5},{5,4},{6,7},{7,6},{8,9},{9,8},{10,11... | collective-permute-start | bytes 786440 | tf_op jit(solution)/shard_map/ppermute | solution.py:371
  22.6 3.6 %copy-start = (f32[8,32,512]{2,1,0:T(8,128)S(1)}, f32[8,32,512]{2,1,0:T(8,128)}, u32[]{:S(2)}) copy-start(f32[8,32,512]{2,1,0:T(8,128)} %q_ref.1) | copy-start | bytes 1572868
  22.6 12.3 %all-to-all-start.1 = ((f32[8,33,2,128]{3,2,1,0:T(2,128)}), f32[8,33,2,128]{3,2,1,0:T(2,128)S(1)}, u32[]{:S(2)}, u32[]{:S(2)}) async-start(f32[8,33,2,128]{3,2,1,0:T(2,128)} %bitcast.5), calls=%async_computation.1 | async-start | bytes 540672 | tf_op jit(solution)/shard_map/all_to_all | solution.py:367

commit v2 on v1

--- a/solution.py
+++ b/solution.py
@@ -45,36 +45,36 @@
     )
 
 
-def pack_kernel(sel_hbm, q_hbm, packed_ref, route_ref, sel_ref, q_ref, sel_sem, q_sem):
+def pack_kernel(
+    sel_hbm, q_hbm, packed_ref, route_ref, sel_ref, found_ref, q_ref, sel_sem, q_sem
+):
     table = pltpu.make_async_copy(sel_hbm, sel_ref, sel_sem)
     table.start()
-    fetch = pltpu.make_async_copy(q_hbm, q_ref, q_sem)
-    fetch.start()
     tiles, rows, _ = q_ref.shape
+    fetches = [
+        pltpu.make_async_copy(q_hbm.at[pl.ds(t, 2)], q_ref.at[pl.ds(t, 2)], q_sem.at[t // 2])
+        for t in range(0, tiles, 2)
+    ]
+    for fetch in fetches:
+        fetch.start()
     span = GROUP * rows + PAD
     shards = packed_ref.shape[0] // span
     picks = sel_ref.shape[0]
     mine = lax.axis_index("ctx")
     for d in range(shards):
-        route_ref[d] = -1
+        found_ref[d] = -1
     table.wait()
-
-    def visit(t, carry):
+    for t in range(tiles):
         for g in range(KEY_VALUE_HEADS):
             for c in range(picks):
                 d = sel_ref[c, g, t]
-
-                @pl.when(d < mine)
-                def _():
-                    route_ref[d] = t * KEY_VALUE_HEADS + g
-
-        return carry
-
-    lax.fori_loop(0, tiles, visit, 0)
-    fetch.wait()
-
-    for d in range(shards):
-        code = jnp.maximum(route_ref[d], 0)
+                found_ref[jnp.where(d < mine, d, shards)] = t * KEY_VALUE_HEADS + g
+    for fetch in fetches:
+        fetch.wait()
+
+    for d in range(shards):
+        route_ref[d] = found_ref[d]
+        code = jnp.maximum(found_ref[d], 0)
         t = code // KEY_VALUE_HEADS
         g = code % KEY_VALUE_HEADS
         for h in range(GROUP):
@@ -153,13 +153,10 @@
     return jnp.sum(jnp.where(row == lane - rows, wide, 0.0), axis=1)
 
 
-def own_kernel(moves, sub_count, q_ref, *refs):
+def own_kernel(moves, sub_count, route_ref, q_ref, *refs):
     count = len(moves)
-    k_refs, v_refs, (base_ref, out_ref, lse_ref) = (
-        refs[:count],
-        refs[count : 2 * count],
-        refs[2 * count :],
-    )
+    k_refs, v_refs, rest = refs[:count], refs[count : 2 * count], refs[2 * count :]
+    base_ref, out_ref, ours_ref, same_ref, flag_ref, lse_ref, code_ref, seen_ref = rest
     tiles, rows, _ = q_ref.shape
     per_head = tiles * rows
     sub = lax.axis_index("sub")
@@ -183,20 +180,50 @@
         lse_ref[:, g, :] = lines
 
 
-def own_pass(moves, sub_count, queries, keys, values):
+    shards = ours_ref.shape[0]
+    blank = seen_ref.shape[1] - 1
+    spots = []
+    for d in range(shards):
+        code = route_ref[d]
+        code_ref[d : d + 1, :] = jnp.full((1, LANES), code, jnp.int32)
+        t = jnp.maximum(code, 0) // KEY_VALUE_HEADS
+        g = jnp.maximum(code, 0) % KEY_VALUE_HEADS
+        ours_ref[d : d + 1, :] = lse_ref[t, pl.ds(g, 1), :]
+        spots.append(jnp.where(code >= 0, code, blank))
+    for d in range(shards):
+        seen_ref[0, spots[shards - 1 - d]] = shards - 1 - d
+        seen_ref[1, spots[d]] = d
+    for d in range(shards):
+        first = (seen_ref[0, spots[d]] == d).astype(jnp.int32)
+        last = (seen_ref[1, spots[d]] == d).astype(jnp.int32)
+        flag_ref[d] = jnp.where(route_ref[d] >= 0, route_ref[d] * 4 + first * 2 + last, -1)
+    codes = code_ref[...]
+    for d in range(shards):
+        match = (codes == code_ref[d : d + 1, :]) & (codes >= 0)
+        same_ref[d] = jnp.where(match, 1.0, 0.0)
+
+
+def own_pass(moves, sub_count, shards, route, queries, keys, values):
     tiles = queries.shape[0]
     return pl.pallas_call(
         functools.partial(own_kernel, moves, sub_count),
         out_shape=(
             jax.ShapeDtypeStruct(queries.shape, jnp.float32),
             jax.ShapeDtypeStruct(queries.shape, jnp.float32),
-            jax.ShapeDtypeStruct((tiles, KEY_VALUE_HEADS, LANES), jnp.float32),
+            jax.ShapeDtypeStruct((shards, LANES), jnp.float32),
+            jax.ShapeDtypeStruct((shards, shards, LANES), jnp.float32),
+            jax.ShapeDtypeStruct((shards,), jnp.int32),
         ),
-        in_specs=[VMEM] * (1 + 2 * len(moves)),
-        out_specs=(VMEM,) * 3,
+        in_specs=[SMEM] + [VMEM] * (1 + 2 * len(moves)),
+        out_specs=(VMEM,) * 4 + (SMEM,),
+        scratch_shapes=[
+            pltpu.VMEM((tiles, KEY_VALUE_HEADS, LANES), jnp.float32),
+            pltpu.VMEM((shards, LANES), jnp.int32),
+            pltpu.SMEM((2, tiles * KEY_VALUE_HEADS + 1), jnp.int32),
+        ],
         compiler_params=PARAMS,
         name="own",
-    )(queries, *keys, *values)
+    )(route, queries, *keys, *values)
 
 
 def others(shards):
@@ -274,83 +301,74 @@
 
 
 def merge_kernel(
-    route_ref, reply_ref, _own, _lse, _base, own_ref, run_ref, out_ref, last_ref, sems
+    flag_vmem, reply_ref, ours_ref, same_ref, _own, _base, own_ref, out_ref, flag_ref, flag_sem, sems
 ):
+    table = pltpu.make_async_copy(flag_vmem, flag_ref, flag_sem)
+    table.start()
     rows = own_ref.shape[1]
     body = GROUP * rows
     span = body + PAD
-    shards = reply_ref.shape[0] // span
+    shards = ours_ref.shape[0]
     width = GROUP * HEAD_SIZE
+    ours = ours_ref[...]
+    lines = [reply_ref[d * span + body : d * span + body + 1, :] for d in range(shards)]
+    match = [same_ref[d] > 0.5 for d in range(shards)]
+    top = ours
+    for d in range(shards):
+        top = jnp.maximum(top, jnp.where(match[d], lines[d], LOW_FILL))
+    w_ours = jnp.exp2(ours - top)
+    total = w_ours
+    for d in range(shards):
+        total = total + jnp.where(match[d], jnp.exp2(lines[d] - top), 0.0)
+    scale = 1.0 / total
+    w_ours = w_ours * scale
+    w_theirs = jnp.exp2(jnp.concatenate(lines, axis=0) - top) * scale
+    row = lax.broadcasted_iota(jnp.int32, (body, LANES), 0)
+    lane = lax.broadcasted_iota(jnp.int32, (body, LANES), 1)
+
+    def stand(line):
+        wide = jnp.where(row == lane, jnp.broadcast_to(line, (body, LANES)), 0.0)
+        return jnp.sum(wide, axis=1, keepdims=True)
+
+    pairs = [(stand(w_ours[d : d + 1]), stand(w_theirs[d : d + 1])) for d in range(shards)]
+
+    table.wait()
+    flags = [flag_ref[d] for d in range(shards)]
 
     def store(d):
-        code = route_ref[d]
+        code = flags[d] // 4
         t = code // KEY_VALUE_HEADS
         columns = pl.ds(pl.multiple_of(code % KEY_VALUE_HEADS * width, width), width)
         return pltpu.make_async_copy(
             own_ref.at[t, :, columns], out_ref.at[t, :, columns], sems.at[d]
         )
 
-    def is_last(d):
-        code = route_ref[d]
-        return (code >= 0) & (last_ref[jnp.maximum(code, 0)] == d)
-
-    def note(d, carry):
-        code = route_ref[d]
-
-        @pl.when(code >= 0)
+    for d in range(shards):
+
+        @pl.when(flags[d] >= 0)
         def _():
-            last_ref[code] = d
-
-        return carry
-
-    lax.fori_loop(0, shards, note, 0)
-    row = lax.broadcasted_iota(jnp.int32, (body, LANES), 0)
-    lane = lax.broadcasted_iota(jnp.int32, (body, LANES), 1)
-
-    def stand(line):
-        wide = jnp.where(row == lane, jnp.broadcast_to(line, (body, LANES)), 0.0)
-        return jnp.sum(wide, axis=1, keepdims=True)
-
-    def visit(d, carry):
-        code = route_ref[d]
-
-        @pl.when(code >= 0)
-        def _():
+            code = flags[d] // 4
             t = code // KEY_VALUE_HEADS
             g = code % KEY_VALUE_HEADS
-            ours = run_ref[t, pl.ds(g, 1), :]
-            theirs = reply_ref[pl.ds(d * span + body, 1), :]
-            top = jnp.maximum(ours, theirs)
-            w_ours = jnp.exp2(ours - top)
-            w_theirs = jnp.exp2(theirs - top)
-            total = w_ours + w_theirs
-            run_ref[t, pl.ds(g, 1), :] = top + jnp.log2(total)
-            a = stand(w_ours / total)
-            b = stand(w_theirs / total)
+            a = jnp.where(flags[d] // 2 % 2 == 1, pairs[d][0], 1.0)
+            b = pairs[d][1]
             for h in range(GROUP):
                 column = pl.ds(pl.multiple_of((g * GROUP + h) * HEAD_SIZE, HEAD_SIZE), HEAD_SIZE)
                 part = slice(h * rows, (h + 1) * rows)
+                start = d * span + h * rows
                 own_ref[t, :, column] = (
-                    a[part] * own_ref[t, :, column]
-                    + b[part] * reply_ref[pl.ds(d * span + h * rows, rows), :]
+                    a[part] * own_ref[t, :, column] + b[part] * reply_ref[start : start + rows, :]
                 )
 
-            @pl.when(last_ref[code] == d)
+            @pl.when(flags[d] % 2 == 1)
             def _():
                 store(d).start()
 
-        return carry
-
-    lax.fori_loop(0, shards, visit, 0)
-
-    def settle(d, carry):
-        @pl.when(is_last(d))
+    for d in range(shards):
+
+        @pl.when((flags[d] >= 0) & (flags[d] % 2 == 1))
         def _():
             store(d).wait()
-
-        return carry
-
-    lax.fori_loop(0, shards, settle, 0)
 
 
 def on_device(queries, keys, values, selected):
@@ -389,9 +407,10 @@
         out_specs=(VMEM, SMEM),
         scratch_shapes=[
             pltpu.SMEM(selected.shape[::-1], jnp.int32),
+            pltpu.SMEM((shards + 1,), jnp.int32),
             pltpu.VMEM(queries.shape, jnp.float32),
             pltpu.SemaphoreType.DMA(()),
-            pltpu.SemaphoreType.DMA(()),
+            pltpu.SemaphoreType.DMA((tiles // 2,)),
         ],
         compiler_params=PARAMS,
         name="pack",
@@ -410,26 +429,26 @@
     all_keys, all_values = near_keys + rest_keys, near_values + rest_values
     reply = routed_pass(shards, arrived, all_keys, all_values)
     answers = exchange(reply)
-    base, own_out, own_lse = own_pass(
-        near_moves + far_moves, sub_count, queries, all_keys, all_values
+    base, own_out, ours, same, flags = own_pass(
+        near_moves + far_moves, sub_count, shards, route, queries, all_keys, all_values
     )
     return pl.pallas_call(
         merge_kernel,
         out_shape=(
             jax.ShapeDtypeStruct(own_out.shape, jnp.float32),
-            jax.ShapeDtypeStruct(own_lse.shape, jnp.float32),
             jax.ShapeDtypeStruct(queries.shape, jnp.float32),
         ),
-        in_specs=[SMEM, VMEM, VMEM, VMEM, HBM],
-        out_specs=(VMEM, VMEM, HBM),
-        input_output_aliases={2: 0, 3: 1, 4: 2},
+        in_specs=[VMEM, VMEM, VMEM, VMEM, VMEM, HBM],
+        out_specs=(VMEM, HBM),
+        input_output_aliases={4: 0, 5: 1},
         scratch_shapes=[
-            pltpu.SMEM((tiles * KEY_VALUE_HEADS,), jnp.int32),
+            pltpu.SMEM((shards,), jnp.int32),
+            pltpu.SemaphoreType.DMA(()),
             pltpu.SemaphoreType.DMA((shards,)),
         ],
         compiler_params=PARAMS,
         name="merge",
-    )(route, answers, own_out, own_lse, base)[2]
+    )(flags, answers, ours, same, own_out, base)[1]
 
 
 def solution(mesh):

time: 36.1 us -> 36 us (level)
  waiting for transfers between devices: 11.8 us -> 11.2 us
  Pallas kernels: 10.2 us -> 10.6 us
    pallas_call x1, Pallas kernels: 4.85 us -> 5.39 us  [own_pass(): pl.pallas_call(functools.partial(own_kernel, moves, sub_count), out_shape...]
    all_to_all x2, waiting for transfers between devices: 8.66 us -> 8.18 us  [exchange(): lax.all_to_all(parted, 'ctx', split_axis=0, concat_axis=0, tiled=True)]
  transfers between devices with their start and end apart: 8 -> 8, of which waited for: 3 -> 3; matrix products, arithmetic and copies ran while one was open for 0% -> 0% of each run, Pallas kernels for 19% -> 20%
where the time goes in v2:
time: 36 us; the launch traced here: 35.6 us
  starting transfers between devices  13.7 us (38%)
  waiting for transfers between devices  11.2 us (31%)
  Pallas kernels  10.6 us (29%)
    all_to_all x2, starting transfers between devices, exchange(): lax.all_to_all(parted, 'ctx', split_axis=0, concat_axis=0, tiled=True)  10.1 us
    all_to_all x2, waiting for transfers between devices, exchange(): lax.all_to_all(parted, 'ctx', split_axis=0, concat_axis=0, tiled=True)  8.18 us
    pallas_call x1, Pallas kernels, own_pass(): pl.pallas_call(functools.partial(own_kernel, moves, sub_count), out_shape...  5.39 us
    ppermute x2, waiting for transfers between devices, shift(): lax.ppermute(x, 'sub', [(s, (s + step * CORES) % sub_count) for s in rang...  3.02 us
    ppermute x2, starting transfers between devices, shift(): lax.ppermute(x, 'sub', [(s, (s + step * CORES) % sub_count) for s in rang...  2.99 us
    pallas_call x1, Pallas kernels, routed_pass(): pl.pallas_call(functools.partial(routed_kernel, count, shards), out_shape...  2.62 us
    pallas_call x1, Pallas kernels, on_device(): pl.pallas_call(pack_kernel, out_shape=(jax.ShapeDtypeStruct((shards * spa...  1.89 us
  transfers between devices with their start and end apart: 8, of which 3 were waited for; matrix products, arithmetic and copies ran while one was open for 0% of the time, Pallas kernels for 20%

profile of v2, /device:TPU:0, one launch (start us, length us, event | category | flops | bytes accessed | tf_op | source)
XLA Modules:
  0.0 35.6 jit_solution(10705576716316639053)
XLA Ops:
  0.0 3.0 %collective-permute-start.1 = (f32[256,256]{1,0:T(8,128)}, f32[256,256]{1,0:T(8,128)S(1)}, u32[]{:S(2)}, u32[]{:S(2)}) collective-permute-start(f32[256,256]{1,0:T(8,128)} %bitcast.9), channel_id=1, source_target_pairs={{0,2},{1,3},{2,0},{3,1},{4,6},{5,7},{6,4},{7,5},{8,10},{9,11},{10,... | collective-permute-start | bytes 786440 | tf_op jit(solution)/shard_map/ppermute | solution.py:392
  3.0 0.0 collective-permute-start.4
  3.0 1.9 %pack.1 = (f32[528,128]{1,0:T(8,128)}, s32[8]{0:T(128)S(1)}) custom-call(s32[3,2,8]{2,1,0:T(2,128)} %bitcast.17, f32[8,32,512]{2,1,0:T(8,128)} %q_ref.1), custom_call_target="tpu_custom_call" | custom-call | tf_op jit(solution)/shard_map/pack/pallas_call | solution.py:400
  4.9 0.0 copy-start.1
  4.9 0.0 copy-start.2
  4.9 6.5 %all-to-all-start = ((f32[8,33,2,128]{3,2,1,0:T(2,128)}), f32[8,33,2,128]{3,2,1,0:T(2,128)S(1)}, u32[]{:S(2)}, u32[]{:S(2)}) async-start(f32[8,33,2,128]{3,2,1,0:T(2,128)} %bitcast.3), calls=%async_computation | async-start | bytes 540672 | tf_op jit(solution)/shard_map/all_to_all | solution.py:385
  11.4 0.0 copy-done.1
  11.4 0.1 collective-permute-start
  11.5 0.0 copy-done.2
  11.5 0.5 %collective-permute-start.3 = (f32[256,256]{1,0:T(8,128)S(1)}, f32[256,256]{1,0:T(8,128)S(1)}, u32[]{:S(2)}, u32[]{:S(2)}) collective-permute-start(f32[256,256]{1,0:T(8,128)S(1)} %bitcast.14), channel_id=1, source_target_pairs={{0,1},{1,0},{2,3},{3,2},{4,5},{5,4},{6,7},{7,6},{8,9},{9,8},{10,11... | collective-permute-start | bytes 786440 | tf_op jit(solution)/shard_map/ppermute | solution.py:389
  12.0 0.0 collective-permute-done.1.refs_2_
  12.0 0.1 collective-permute-start.2
  12.1 3.0 %collective-permute-done.4.refs_6_ = f32[256,256]{1,0:T(8,128)S(1)} collective-permute-done((f32[256,256]{1,0:T(8,128)}, f32[256,256]{1,0:T(8,128)S(1)}, u32[]{:S(2)}, u32[]{:S(2)}) %collective-permute-start.4) | collective-permute-done | bytes 262176 | tf_op jit(solution)/shard_map/ppermute | solution.py:392
  15.1 0.0 collective-permute-start.5
  15.1 0.0 collective-permute-done.refs_1_
  15.1 0.0 collective-permute-done.3.refs_5_
  15.1 4.9 %all-to-all-done = f32[8,33,2,128]{3,2,1,0:T(2,128)S(1)} async-done(((f32[8,33,2,128]{3,2,1,0:T(2,128)}), f32[8,33,2,128]{3,2,1,0:T(2,128)S(1)}, u32[]{:S(2)}, u32[]{:S(2)}) %all-to-all-start) | async-done | bytes 270368 | tf_op jit(solution)/shard_map/all_to_all | solution.py:385
  20.1 0.0 collective-permute-done.2.refs_3_
  20.1 0.0 collective-permute-done.5.refs_7_
  20.1 2.6 %routed.1 = f32[528,128]{1,0:T(8,128)} custom-call(f32[528,128]{1,0:T(8,128)S(1)} %bitcast.7, f32[256,256]{1,0:T(8,128)S(1)} %bitcast.11, f32[256,256]{1,0:T(8,128)S(1)} %collective-permute-done.refs_1_, f32[256,256]{1,0:T(8,128)S(1)} %collective-permute-done.1.refs_2_, f32[256,256]{1,0:T(8,128)S(1)} %collective-permute-done.2.refs_3_, ...), custom_call_target="tpu_custom_call" | custom-call | tf_op jit(solution)/shard_map/routed/pallas_call | solution.py:293
  22.7 0.0 copy-start
  22.7 3.6 %all-to-all-start.1 = ((f32[8,33,2,128]{3,2,1,0:T(2,128)}), f32[8,33,2,128]{3,2,1,0:T(2,128)S(1)}, u32[]{:S(2)}, u32[]{:S(2)}) async-start(f32[8,33,2,128]{3,2,1,0:T(2,128)} %bitcast.5), calls=%async_computation.1 | async-start | bytes 540672 | tf_op jit(solution)/shard_map/all_to_all | solution.py:385
  26.3 0.0 copy-done
  26.3 5.4 %own.1 = (f32[8,32,512]{2,1,0:T(8,128)}, f32[8,32,512]{2,1,0:T(8,128)S(1)}, f32[8,128]{1,0:T(8,128)S(1)}, f32[8,8,128]{2,1,0:T(8,128)S(1)}, s32[8]{0:T(128)S(1)}) custom-call(s32[8]{0:T(128)S(1)} %get-tuple-element.13.route_ref, f32[8,32,512]{2,1,0:T(8,128)S(1)} %copy-done, f32[256,256]{1,0:T(8,128)S(1)} %bitcast.12, ...), custom_call_target="tpu_custom_call" | custom-call | tf_op jit(solution)/shard_map/own/pallas_call | solution.py:208
  31.7 3.2 %all-to-all-done.1 = f32[8,33,2,128]{3,2,1,0:T(2,128)S(1)} async-done(((f32[8,33,2,128]{3,2,1,0:T(2,128)}), f32[8,33,2,128]{3,2,1,0:T(2,128)S(1)}, u32[]{:S(2)}, u32[]{:S(2)}) %all-to-all-start.1) | async-done | bytes 270368 | tf_op jit(solution)/shard_map/all_to_all | solution.py:385
  34.9 0.7 %merge.1 = (f32[8,32,512]{2,1,0:T(8,128)S(1)}, f32[8,32,512]{2,1,0:T(8,128)}) custom-call(s32[8]{0:T(128)S(1)} %get-tuple-element.14.flag_vmem, f32[528,128]{1,0:T(8,128)S(1)} %bitcast.8, f32[8,128]{1,0:T(8,128)S(1)} %get-tuple-element.16.ours_ref, f32[8,8,128]{2,1,0:T(8,128)S(1)} %get-tuple-element.17.same_ref, ...), custom_call_target="tpu_custom_call", output_to_operand_aliasing={{0}: (4, {}), {1}: (5, {})} | custom-call | tf_op jit(solution)/shard_map/merge/pallas_call | solution.py:435
Async XLA Ops:
  0.0 12.0 %collective-permute-start.1 = (f32[256,256]{1,0:T(8,128)}, f32[256,256]{1,0:T(8,128)S(1)}, u32[]{:S(2)}, u32[]{:S(2)}) collective-permute-start(f32[256,256]{1,0:T(8,128)} %bitcast.9), channel_id=1, source_target_pairs={{0,2},{1,3},{2,0},{3,1},{4,6},{5,7},{6,4},{7,5},{8,10},{9,11},{10,... | collective-permute-start | bytes 786440 | tf_op jit(solution)/shard_map/ppermute | solution.py:392
  3.0 12.1 %collective-permute-start.4 = (f32[256,256]{1,0:T(8,128)}, f32[256,256]{1,0:T(8,128)S(1)}, u32[]{:S(2)}, u32[]{:S(2)}) collective-permute-start(f32[256,256]{1,0:T(8,128)} %bitcast.13), channel_id=1, source_target_pairs={{0,2},{1,3},{2,0},{3,1},{4,6},{5,7},{6,4},{7,5},{8,10},{9,11},{10,... | collective-permute-start | bytes 786440 | tf_op jit(solution)/shard_map/ppermute | solution.py:392
  4.9 6.5 %copy-start.1 = (f32[1,256,256]{2,1,0:T(8,128)S(1)}, f32[1,256,256]{2,1,0:T(8,128)}, u32[]{:S(2)}) copy-start(f32[1,256,256]{2,1,0:T(8,128)} %param.5) | copy-start | bytes 786436
  4.9 6.6 %copy-start.2 = (f32[1,256,256]{2,1,0:T(8,128)S(1)}, f32[1,256,256]{2,1,0:T(8,128)}, u32[]{:S(2)}) copy-start(f32[1,256,256]{2,1,0:T(8,128)} %param.6) | copy-start | bytes 786436
  4.9 15.1 %all-to-all-start = ((f32[8,33,2,128]{3,2,1,0:T(2,128)}), f32[8,33,2,128]{3,2,1,0:T(2,128)S(1)}, u32[]{:S(2)}, u32[]{:S(2)}) async-start(f32[8,33,2,128]{3,2,1,0:T(2,128)} %bitcast.3), calls=%async_computation | async-start | bytes 540672 | tf_op jit(solution)/shard_map/all_to_all | solution.py:385
  11.4 3.7 %collective-permute-start = (f32[256,256]{1,0:T(8,128)S(1)}, f32[256,256]{1,0:T(8,128)S(1)}, u32[]{:S(2)}, u32[]{:S(2)}) collective-permute-start(f32[256,256]{1,0:T(8,128)S(1)} %bitcast.10), channel_id=1, source_target_pairs={{0,1},{1,0},{2,3},{3,2},{4,5},{5,4},{6,7},{7,6},{8,9},{9,8},{10,11... | collective-permute-start | bytes 786440 | tf_op jit(solution)/shard_map/ppermute | solution.py:389
  11.5 3.6 %collective-permute-start.3 = (f32[256,256]{1,0:T(8,128)S(1)}, f32[256,256]{1,0:T(8,128)S(1)}, u32[]{:S(2)}, u32[]{:S(2)}) collective-permute-start(f32[256,256]{1,0:T(8,128)S(1)} %bitcast.14), channel_id=1, source_target_pairs={{0,1},{1,0},{2,3},{3,2},{4,5},{5,4},{6,7},{7,6},{8,9},{9,8},{10,11... | collective-permute-start | bytes 786440 | tf_op jit(solution)/shard_map/ppermute | solution.py:389
  12.0 8.1 %collective-permute-start.2 = (f32[256,256]{1,0:T(8,128)S(1)}, f32[256,256]{1,0:T(8,128)S(1)}, u32[]{:S(2)}, u32[]{:S(2)}) collective-permute-start(f32[256,256]{1,0:T(8,128)S(1)} %collective-permute-done.1.refs_2_), channel_id=1, source_target_pairs={{0,1},{1,0},{2,3},{3,2},{4,5},{5,4},{6,7},{7,6},{8,9},{9,8},{10,11... | collective-permute-start | bytes 786440 | tf_op jit(solution)/shard_map/ppermute | solution.py:389
  15.1 5.0 %collective-permute-start.5 = (f32[256,256]{1,0:T(8,128)S(1)}, f32[256,256]{1,0:T(8,128)S(1)}, u32[]{:S(2)}, u32[]{:S(2)}) collective-permute-start(f32[256,256]{1,0:T(8,128)S(1)} %collective-permute-done.4.refs_6_), channel_id=1, source_target_pairs={{0,1},{1,0},{2,3},{3,2},{4,5},{5,4},{6,7},{7,6},{8,9},{9,8},{10,11... | collective-permute-start | bytes 786440 | tf_op jit(solution)/shard_map/ppermute | solution.py:389
  22.7 3.6 %copy-start = (f32[8,32,512]{2,1,0:T(8,128)S(1)}, f32[8,32,512]{2,1,0:T(8,128)}, u32[]{:S(2)}) copy-start(f32[8,32,512]{2,1,0:T(8,128)} %q_ref.1) | copy-start | bytes 1572868
  22.7 12.3 %all-to-all-start.1 = ((f32[8,33,2,128]{3,2,1,0:T(2,128)}), f32[8,33,2,128]{3,2,1,0:T(2,128)S(1)}, u32[]{:S(2)}, u32[]{:S(2)}) async-start(f32[8,33,2,128]{3,2,1,0:T(2,128)} %bitcast.5), calls=%async_computation.1 | async-start | bytes 540672 | tf_op jit(solution)/shard_map/all_to_all | solution.py:385

commit v3 on v2

--- a/solution.py
+++ b/solution.py
@@ -3,6 +3,7 @@
 
 import jax
 import jax.numpy as jnp
+import numpy as np
 from jax import lax
 from jax.experimental import pallas as pl
 from jax.experimental.pallas import tpu as pltpu
@@ -16,6 +17,8 @@
 CORES = 2
 LANES = 128
 PAD = 2
+SEND_LEAD = 0.5
+REPLY_LEAD = 0.5
 
 LOW_FILL = -1e30
 SCALE = HEAD_SIZE ** (-0.5) * math.log2(math.e)
@@ -25,6 +28,10 @@
 SMEM = pl.BlockSpec(memory_space=pltpu.SMEM)
 HBM = pl.BlockSpec(memory_space=pltpu.HBM)
 PARAMS = pltpu.CompilerParams(vmem_limit_bytes=24 * 1024 * 1024)
+
+
+def spot_of(d, lead, shards):
+    return (d + shards - int(lead * shards)) % shards
 
 
 def halves(x):
@@ -79,10 +86,11 @@
         g = code % KEY_VALUE_HEADS
         for h in range(GROUP):
             column = pl.multiple_of((g * GROUP + h) * HEAD_SIZE, HEAD_SIZE)
-            start = d * span + h * rows
+            start = spot_of(d, SEND_LEAD, shards) * span + h * rows
             packed_ref[start : start + rows, :] = q_ref[t, :, pl.ds(column, HEAD_SIZE)]
         label = jnp.full((PAD, LANES), g, jnp.int32).astype(jnp.float32)
-        packed_ref[d * span + GROUP * rows : (d + 1) * span, :] = label
+        end = (spot_of(d, SEND_LEAD, shards) + 1) * span
+        packed_ref[end - PAD : end, :] = label
 
 
 def source_of(sub, move, sub_count):
@@ -253,8 +261,9 @@
     span = packed_ref.shape[0] // shards
     body = span - PAD
     slots = others(shards)
-    label = labels_of(packed_ref, slots, body)
-    rows = jnp.concatenate([packed_ref[pl.ds(j * span, body), :] for j in slots], axis=0) * SCALE
+    places = [spot_of(j, SEND_LEAD, shards) for j in slots]
+    label = labels_of(packed_ref, places, body)
+    rows = jnp.concatenate([packed_ref[pl.ds(j * span, body), :] for j in places], axis=0) * SCALE
     wide = jnp.concatenate(
         [jnp.where(label == g, rows, 0.0) for g in range(KEY_VALUE_HEADS)], axis=1
     )
@@ -283,7 +292,8 @@
     scale = 1.0 / total
     out = sum(shrink * scale * part[2] for shrink, part in zip(shrinks, parts))
     lines = lines_of(top + jnp.log2(total), shards - 1, 0)
-    for i, j in enumerate(slots):
+    for i, slot in enumerate(slots):
+        j = spot_of(slot, REPLY_LEAD, shards)
         reply_ref[pl.ds(j * span, body), :] = out[i * body : (i + 1) * body]
         reply_ref[pl.ds(j * span + body, PAD), :] = jnp.broadcast_to(lines[i : i + 1], (PAD, LANES))
 
@@ -311,7 +321,8 @@
     shards = ours_ref.shape[0]
     width = GROUP * HEAD_SIZE
     ours = ours_ref[...]
-    lines = [reply_ref[d * span + body : d * span + body + 1, :] for d in range(shards)]
+    spots = [spot_of(d, REPLY_LEAD, shards) * span for d in range(shards)]
+    lines = [reply_ref[spot + body : spot + body + 1, :] for spot in spots]
     match = [same_ref[d] > 0.5 for d in range(shards)]
     top = ours
     for d in range(shards):
@@ -355,7 +366,7 @@
             for h in range(GROUP):
                 column = pl.ds(pl.multiple_of((g * GROUP + h) * HEAD_SIZE, HEAD_SIZE), HEAD_SIZE)
                 part = slice(h * rows, (h + 1) * rows)
-                start = d * span + h * rows
+                start = spots[d] + h * rows
                 own_ref[t, :, column] = (
                     a[part] * own_ref[t, :, column] + b[part] * reply_ref[start : start + rows, :]
                 )
@@ -380,9 +391,12 @@
     keys = keys.reshape(keys.shape[1:])
     values = values.reshape(values.shape[1:])
 
-    def exchange(x):
+    def exchange(x, lead):
+        order = [int(i) for i in np.argsort([spot_of(d, lead, shards) for d in range(shards)])]
         parted = x.reshape(shards, span // PAD, PAD, LANES)
-        moved = lax.all_to_all(parted, "ctx", split_axis=0, concat_axis=0, tiled=True)
+        moved = lax.all_to_all(
+            parted, "ctx", split_axis=0, concat_axis=0, tiled=True, axis_index_groups=[order]
+        )
         return moved.reshape(x.shape)
 
     def swap(x):
@@ -418,7 +432,7 @@
         pltpu.with_memory_space_constraint(jnp.transpose(selected, (2, 1, 0)), pltpu.HBM),
         pltpu.with_memory_space_constraint(queries, pltpu.HBM),
     )
-    arrived = exchange(packed)
+    arrived = exchange(packed, SEND_LEAD)
 
     near_moves = ((0, False), (0, True))
     far_moves = tuple((step, swapped) for step in range(1, chips) for swapped in (False, True))
@@ -428,7 +442,7 @@
         rest_values += [far_value, swap(far_value)]
     all_keys, all_values = near_keys + rest_keys, near_values + rest_values
     reply = routed_pass(shards, arrived, all_keys, all_values)
-    answers = exchange(reply)
+    answers = exchange(reply, REPLY_LEAD)
     base, own_out, ours, same, flags = own_pass(
         near_moves + far_moves, sub_count, shards, route, queries, all_keys, all_values
     )

time: 36 us -> 34.1 us (0.947)
  waiting for transfers between devices: 11.2 us -> 6.95 us
  starting transfers between devices: 13.7 us -> 16.1 us
    all_to_all x2, waiting for transfers between devices: 8.18 us -> 4.41 us  [exchange(): lax.all_to_all(parted, 'ctx', split_axis=0, concat_axis=0, tiled=True, ax...]
    all_to_all x2, starting transfers between devices: 10.1 us -> 12.5 us  [exchange(): lax.all_to_all(parted, 'ctx', split_axis=0, concat_axis=0, tiled=True, ax...]
    ppermute x2, waiting for transfers between devices: 3.02 us -> 2.54 us  [shift(): lax.ppermute(x, 'sub', [(s, (s + step * CORES) % sub_count) for s in rang...]
  transfers between devices with their start and end apart: 8 -> 8, of which waited for: 3 -> 3; matrix products, arithmetic and copies ran while one was open for 0% -> 0% of each run, Pallas kernels for 20% -> 22%
where the time goes in v3:
time: 34.1 us; the launch traced here: 33.7 us
  starting transfers between devices  16.1 us (47%)
  Pallas kernels  10.6 us (31%)
  waiting for transfers between devices  6.95 us (20%)
    all_to_all x2, starting transfers between devices, exchange(): lax.all_to_all(parted, 'ctx', split_axis=0, concat_axis=0, tiled=True, ax...  12.5 us
    pallas_call x1, Pallas kernels, own_pass(): pl.pallas_call(functools.partial(own_kernel, moves, sub_count), out_shape...  5.38 us
    all_to_all x2, waiting for transfers between devices, exchange(): lax.all_to_all(parted, 'ctx', split_axis=0, concat_axis=0, tiled=True, ax...  4.41 us
    ppermute x2, starting transfers between devices, shift(): lax.ppermute(x, 'sub', [(s, (s + step * CORES) % sub_count) for s in rang...  2.99 us
    pallas_call x1, Pallas kernels, routed_pass(): pl.pallas_call(functools.partial(routed_kernel, count, shards), out_shape...  2.61 us
    ppermute x2, waiting for transfers between devices, shift(): lax.ppermute(x, 'sub', [(s, (s + step * CORES) % sub_count) for s in rang...  2.54 us
    pallas_call x1, Pallas kernels, on_device(): pl.pallas_call(pack_kernel, out_shape=(jax.ShapeDtypeStruct((shards * spa...  1.89 us
    pallas_call x1, Pallas kernels, on_device(): pl.pallas_call(merge_kernel, out_shape=(jax.ShapeDtypeStruct(own_out.shap...  0.72 us
  transfers between devices with their start and end apart: 8, of which 3 were waited for; matrix products, arithmetic and copies ran while one was open for 0% of the time, Pallas kernels for 22%

profile of v3, /device:TPU:0, one launch (start us, length us, event | category | flops | bytes accessed | tf_op | source)
XLA Modules:
  0.0 33.7 jit_solution(13697694276576996640)
XLA Ops:
  0.0 3.0 %collective-permute-start.1 = (f32[256,256]{1,0:T(8,128)}, f32[256,256]{1,0:T(8,128)S(1)}, u32[]{:S(2)}, u32[]{:S(2)}) collective-permute-start(f32[256,256]{1,0:T(8,128)} %bitcast.9), channel_id=1, source_target_pairs={{0,2},{1,3},{2,0},{3,1},{4,6},{5,7},{6,4},{7,5},{8,10},{9,11},{10,... | collective-permute-start | bytes 786440 | tf_op jit(solution)/shard_map/ppermute | solution.py:406
  3.0 0.0 collective-permute-start.4
  3.0 1.9 %pack.1 = (f32[528,128]{1,0:T(8,128)}, s32[8]{0:T(128)S(1)}) custom-call(s32[3,2,8]{2,1,0:T(2,128)} %bitcast.17, f32[8,32,512]{2,1,0:T(8,128)} %q_ref.1), custom_call_target="tpu_custom_call" | custom-call | tf_op jit(solution)/shard_map/pack/pallas_call | solution.py:414
  4.9 0.0 copy-start.1
  4.9 0.0 copy-start.2
  4.9 7.0 %all-to-all-start = ((f32[8,33,2,128]{3,2,1,0:T(2,128)}), f32[8,33,2,128]{3,2,1,0:T(2,128)S(1)}, u32[]{:S(2)}, u32[]{:S(2)}) async-start(f32[8,33,2,128]{3,2,1,0:T(2,128)} %bitcast.3), calls=%async_computation | async-start | bytes 540672 | tf_op jit(solution)/shard_map/all_to_all | solution.py:397
  12.0 0.0 copy-done.1
  12.0 0.0 collective-permute-start
  12.0 0.0 copy-done.2
  12.0 0.5 %collective-permute-start.3 = (f32[256,256]{1,0:T(8,128)S(1)}, f32[256,256]{1,0:T(8,128)S(1)}, u32[]{:S(2)}, u32[]{:S(2)}) collective-permute-start(f32[256,256]{1,0:T(8,128)S(1)} %bitcast.14), channel_id=1, source_target_pairs={{0,1},{1,0},{2,3},{3,2},{4,5},{5,4},{6,7},{7,6},{8,9},{9,8},{10,11... | collective-permute-start | bytes 786440 | tf_op jit(solution)/shard_map/ppermute | solution.py:403
  12.5 0.0 collective-permute-done.1.refs_2_
  12.5 0.1 collective-permute-start.2
  12.6 2.5 %collective-permute-done.4.refs_6_ = f32[256,256]{1,0:T(8,128)S(1)} collective-permute-done((f32[256,256]{1,0:T(8,128)}, f32[256,256]{1,0:T(8,128)S(1)}, u32[]{:S(2)}, u32[]{:S(2)}) %collective-permute-start.4) | collective-permute-done | bytes 262176 | tf_op jit(solution)/shard_map/ppermute | solution.py:406
  15.1 0.0 collective-permute-start.5
  15.1 0.0 collective-permute-done.refs_1_
  15.1 0.0 collective-permute-done.3.refs_5_
  15.1 3.0 %all-to-all-done = f32[8,33,2,128]{3,2,1,0:T(2,128)S(1)} async-done(((f32[8,33,2,128]{3,2,1,0:T(2,128)}), f32[8,33,2,128]{3,2,1,0:T(2,128)S(1)}, u32[]{:S(2)}, u32[]{:S(2)}) %all-to-all-start) | async-done | bytes 270368 | tf_op jit(solution)/shard_map/all_to_all | solution.py:397
  18.1 0.0 collective-permute-done.2.refs_3_
  18.1 0.0 collective-permute-done.5.refs_7_
  18.1 2.6 %routed.1 = f32[528,128]{1,0:T(8,128)} custom-call(f32[528,128]{1,0:T(8,128)S(1)} %bitcast.7, f32[256,256]{1,0:T(8,128)S(1)} %bitcast.11, f32[256,256]{1,0:T(8,128)S(1)} %collective-permute-done.refs_1_, f32[256,256]{1,0:T(8,128)S(1)} %collective-permute-done.1.refs_2_, f32[256,256]{1,0:T(8,128)S(1)} %collective-permute-done.2.refs_3_, ...), custom_call_target="tpu_custom_call" | custom-call | tf_op jit(solution)/shard_map/routed/pallas_call | solution.py:303
  20.7 0.0 copy-start
  20.7 5.5 %all-to-all-start.1 = ((f32[8,33,2,128]{3,2,1,0:T(2,128)}), f32[8,33,2,128]{3,2,1,0:T(2,128)S(1)}, u32[]{:S(2)}, u32[]{:S(2)}) async-start(f32[8,33,2,128]{3,2,1,0:T(2,128)} %bitcast.5), calls=%async_computation.1 | async-start | bytes 540672 | tf_op jit(solution)/shard_map/all_to_all | solution.py:397
  26.2 0.0 copy-done
  26.2 5.4 %own.1 = (f32[8,32,512]{2,1,0:T(8,128)}, f32[8,32,512]{2,1,0:T(8,128)S(1)}, f32[8,128]{1,0:T(8,128)S(1)}, f32[8,8,128]{2,1,0:T(8,128)S(1)}, s32[8]{0:T(128)S(1)}) custom-call(s32[8]{0:T(128)S(1)} %get-tuple-element.13.route_ref, f32[8,32,512]{2,1,0:T(8,128)S(1)} %copy-done, f32[256,256]{1,0:T(8,128)S(1)} %bitcast.12, ...), custom_call_target="tpu_custom_call" | custom-call | tf_op jit(solution)/shard_map/own/pallas_call | solution.py:216
  31.6 1.4 %all-to-all-done.1 = f32[8,33,2,128]{3,2,1,0:T(2,128)S(1)} async-done(((f32[8,33,2,128]{3,2,1,0:T(2,128)}), f32[8,33,2,128]{3,2,1,0:T(2,128)S(1)}, u32[]{:S(2)}, u32[]{:S(2)}) %all-to-all-start.1) | async-done | bytes 270368 | tf_op jit(solution)/shard_map/all_to_all | solution.py:397
  33.0 0.7 %merge.1 = (f32[8,32,512]{2,1,0:T(8,128)S(1)}, f32[8,32,512]{2,1,0:T(8,128)}) custom-call(s32[8]{0:T(128)S(1)} %get-tuple-element.14.flag_vmem, f32[528,128]{1,0:T(8,128)S(1)} %bitcast.8, f32[8,128]{1,0:T(8,128)S(1)} %get-tuple-element.16.ours_ref, f32[8,8,128]{2,1,0:T(8,128)S(1)} %get-tuple-element.17.same_ref, ...), custom_call_target="tpu_custom_call", output_to_operand_aliasing={{0}: (4, {}), {1}: (5, {})} | custom-call | tf_op jit(solution)/shard_map/merge/pallas_call | solution.py:449
Async XLA Ops:
  0.0 12.5 %collective-permute-start.1 = (f32[256,256]{1,0:T(8,128)}, f32[256,256]{1,0:T(8,128)S(1)}, u32[]{:S(2)}, u32[]{:S(2)}) collective-permute-start(f32[256,256]{1,0:T(8,128)} %bitcast.9), channel_id=1, source_target_pairs={{0,2},{1,3},{2,0},{3,1},{4,6},{5,7},{6,4},{7,5},{8,10},{9,11},{10,... | collective-permute-start | bytes 786440 | tf_op jit(solution)/shard_map/ppermute | solution.py:406
  3.0 12.1 %collective-permute-start.4 = (f32[256,256]{1,0:T(8,128)}, f32[256,256]{1,0:T(8,128)S(1)}, u32[]{:S(2)}, u32[]{:S(2)}) collective-permute-start(f32[256,256]{1,0:T(8,128)} %bitcast.13), channel_id=1, source_target_pairs={{0,2},{1,3},{2,0},{3,1},{4,6},{5,7},{6,4},{7,5},{8,10},{9,11},{10,... | collective-permute-start | bytes 786440 | tf_op jit(solution)/shard_map/ppermute | solution.py:406
  4.9 7.1 %copy-start.1 = (f32[1,256,256]{2,1,0:T(8,128)S(1)}, f32[1,256,256]{2,1,0:T(8,128)}, u32[]{:S(2)}) copy-start(f32[1,256,256]{2,1,0:T(8,128)} %param.5) | copy-start | bytes 786436
  4.9 7.1 %copy-start.2 = (f32[1,256,256]{2,1,0:T(8,128)S(1)}, f32[1,256,256]{2,1,0:T(8,128)}, u32[]{:S(2)}) copy-start(f32[1,256,256]{2,1,0:T(8,128)} %param.6) | copy-start | bytes 786436
  4.9 13.2 %all-to-all-start = ((f32[8,33,2,128]{3,2,1,0:T(2,128)}), f32[8,33,2,128]{3,2,1,0:T(2,128)S(1)}, u32[]{:S(2)}, u32[]{:S(2)}) async-start(f32[8,33,2,128]{3,2,1,0:T(2,128)} %bitcast.3), calls=%async_computation | async-start | bytes 540672 | tf_op jit(solution)/shard_map/all_to_all | solution.py:397
  12.0 3.1 %collective-permute-start = (f32[256,256]{1,0:T(8,128)S(1)}, f32[256,256]{1,0:T(8,128)S(1)}, u32[]{:S(2)}, u32[]{:S(2)}) collective-permute-start(f32[256,256]{1,0:T(8,128)S(1)} %bitcast.10), channel_id=1, source_target_pairs={{0,1},{1,0},{2,3},{3,2},{4,5},{5,4},{6,7},{7,6},{8,9},{9,8},{10,11... | collective-permute-start | bytes 786440 | tf_op jit(solution)/shard_map/ppermute | solution.py:403
  12.0 3.1 %collective-permute-start.3 = (f32[256,256]{1,0:T(8,128)S(1)}, f32[256,256]{1,0:T(8,128)S(1)}, u32[]{:S(2)}, u32[]{:S(2)}) collective-permute-start(f32[256,256]{1,0:T(8,128)S(1)} %bitcast.14), channel_id=1, source_target_pairs={{0,1},{1,0},{2,3},{3,2},{4,5},{5,4},{6,7},{7,6},{8,9},{9,8},{10,11... | collective-permute-start | bytes 786440 | tf_op jit(solution)/shard_map/ppermute | solution.py:403
  12.5 5.6 %collective-permute-start.2 = (f32[256,256]{1,0:T(8,128)S(1)}, f32[256,256]{1,0:T(8,128)S(1)}, u32[]{:S(2)}, u32[]{:S(2)}) collective-permute-start(f32[256,256]{1,0:T(8,128)S(1)} %collective-permute-done.1.refs_2_), channel_id=1, source_target_pairs={{0,1},{1,0},{2,3},{3,2},{4,5},{5,4},{6,7},{7,6},{8,9},{9,8},{10,11... | collective-permute-start | bytes 786440 | tf_op jit(solution)/shard_map/ppermute | solution.py:403
  15.1 3.0 %collective-permute-start.5 = (f32[256,256]{1,0:T(8,128)S(1)}, f32[256,256]{1,0:T(8,128)S(1)}, u32[]{:S(2)}, u32[]{:S(2)}) collective-permute-start(f32[256,256]{1,0:T(8,128)S(1)} %collective-permute-done.4.refs_6_), channel_id=1, source_target_pairs={{0,1},{1,0},{2,3},{3,2},{4,5},{5,4},{6,7},{7,6},{8,9},{9,8},{10,11... | collective-permute-start | bytes 786440 | tf_op jit(solution)/shard_map/ppermute | solution.py:403
  20.7 5.5 %copy-start = (f32[8,32,512]{2,1,0:T(8,128)S(1)}, f32[8,32,512]{2,1,0:T(8,128)}, u32[]{:S(2)}) copy-start(f32[8,32,512]{2,1,0:T(8,128)} %q_ref.1) | copy-start | bytes 1572868
  20.7 12.3 %all-to-all-start.1 = ((f32[8,33,2,128]{3,2,1,0:T(2,128)}), f32[8,33,2,128]{3,2,1,0:T(2,128)S(1)}, u32[]{:S(2)}, u32[]{:S(2)}) async-start(f32[8,33,2,128]{3,2,1,0:T(2,128)} %bitcast.5), calls=%async_computation.1 | async-start | bytes 540672 | tf_op jit(solution)/shard_map/all_to_all | solution.py:397

commit v4 on v3

--- a/solution.py
+++ b/solution.py
@@ -52,8 +52,21 @@
     )
 
 
+def find_routes(sel_ref, found_ref):
+    picks, groups, tiles = sel_ref.shape
+    shards = found_ref.shape[0] - 1
+    mine = lax.axis_index("ctx")
+    for d in range(shards):
+        found_ref[d] = -1
+    for t in range(tiles):
+        for g in range(groups):
+            for c in range(picks):
+                d = sel_ref[c, g, t]
+                found_ref[jnp.where(d < mine, d, shards)] = t * groups + g
+
+
 def pack_kernel(
-    sel_hbm, q_hbm, packed_ref, route_ref, sel_ref, found_ref, q_ref, sel_sem, q_sem
+    sel_hbm, q_hbm, packed_ref, sel_ref, found_ref, q_ref, sel_sem, q_sem
 ):
     table = pltpu.make_async_copy(sel_hbm, sel_ref, sel_sem)
     table.start()
@@ -66,21 +79,12 @@
         fetch.start()
     span = GROUP * rows + PAD
     shards = packed_ref.shape[0] // span
-    picks = sel_ref.shape[0]
-    mine = lax.axis_index("ctx")
-    for d in range(shards):
-        found_ref[d] = -1
     table.wait()
-    for t in range(tiles):
-        for g in range(KEY_VALUE_HEADS):
-            for c in range(picks):
-                d = sel_ref[c, g, t]
-                found_ref[jnp.where(d < mine, d, shards)] = t * KEY_VALUE_HEADS + g
+    find_routes(sel_ref, found_ref)
     for fetch in fetches:
         fetch.wait()
 
     for d in range(shards):
-        route_ref[d] = found_ref[d]
         code = jnp.maximum(found_ref[d], 0)
         t = code // KEY_VALUE_HEADS
         g = code % KEY_VALUE_HEADS
@@ -161,10 +165,13 @@
     return jnp.sum(jnp.where(row == lane - rows, wide, 0.0), axis=1)
 
 
-def own_kernel(moves, sub_count, route_ref, q_ref, *refs):
+def own_kernel(moves, sub_count, sel_hbm, q_ref, *refs):
     count = len(moves)
     k_refs, v_refs, rest = refs[:count], refs[count : 2 * count], refs[2 * count :]
-    base_ref, out_ref, ours_ref, same_ref, flag_ref, lse_ref, code_ref, seen_ref = rest
+    base_ref, out_ref, ours_ref, same_ref, flag_ref, *scratch = rest
+    lse_ref, code_ref, seen_ref, sel_ref, route_ref, sel_sem = scratch
+    table = pltpu.make_async_copy(sel_hbm, sel_ref, sel_sem)
+    table.start()
     tiles, rows, _ = q_ref.shape
     per_head = tiles * rows
     sub = lax.axis_index("sub")
@@ -188,6 +195,8 @@
         lse_ref[:, g, :] = lines
 
 
+    table.wait()
+    find_routes(sel_ref, route_ref)
     shards = ours_ref.shape[0]
     blank = seen_ref.shape[1] - 1
     spots = []
@@ -211,7 +220,7 @@
         same_ref[d] = jnp.where(match, 1.0, 0.0)
 
 
-def own_pass(moves, sub_count, shards, route, queries, keys, values):
+def own_pass(moves, sub_count, shards, table, queries, keys, values):
     tiles = queries.shape[0]
     return pl.pallas_call(
         functools.partial(own_kernel, moves, sub_count),
@@ -222,16 +231,19 @@
             jax.ShapeDtypeStruct((shards, shards, LANES), jnp.float32),
             jax.ShapeDtypeStruct((shards,), jnp.int32),
         ),
-        in_specs=[SMEM] + [VMEM] * (1 + 2 * len(moves)),
+        in_specs=[HBM] + [VMEM] * (1 + 2 * len(moves)),
         out_specs=(VMEM,) * 4 + (SMEM,),
         scratch_shapes=[
             pltpu.VMEM((tiles, KEY_VALUE_HEADS, LANES), jnp.float32),
             pltpu.VMEM((shards, LANES), jnp.int32),
             pltpu.SMEM((2, tiles * KEY_VALUE_HEADS + 1), jnp.int32),
+            pltpu.SMEM(table.shape, jnp.int32),
+            pltpu.SMEM((shards + 1,), jnp.int32),
+            pltpu.SemaphoreType.DMA(()),
         ],
         compiler_params=PARAMS,
         name="own",
-    )(route, queries, *keys, *values)
+    )(table, queries, *keys, *values)
 
 
 def others(shards):
@@ -411,14 +423,12 @@
     far_values = [shift(values, step) for step in range(1, chips)]
     near_keys, near_values = [keys, swap(keys)], [values, swap(values)]
 
-    packed, route = pl.pallas_call(
+    table = pltpu.with_memory_space_constraint(jnp.transpose(selected, (2, 1, 0)), pltpu.HBM)
+    packed = pl.pallas_call(
         pack_kernel,
-        out_shape=(
-            jax.ShapeDtypeStruct((shards * span, LANES), jnp.float32),
-            jax.ShapeDtypeStruct((shards,), jnp.int32),
-        ),
+        out_shape=jax.ShapeDtypeStruct((shards * span, LANES), jnp.float32),
         in_specs=[HBM, HBM],
-        out_specs=(VMEM, SMEM),
+        out_specs=VMEM,
         scratch_shapes=[
             pltpu.SMEM(selected.shape[::-1], jnp.int32),
             pltpu.SMEM((shards + 1,), jnp.int32),
@@ -429,7 +439,7 @@
         compiler_params=PARAMS,
         name="pack",
     )(
-        pltpu.with_memory_space_constraint(jnp.transpose(selected, (2, 1, 0)), pltpu.HBM),
+        table,
         pltpu.with_memory_space_constraint(queries, pltpu.HBM),
     )
     arrived = exchange(packed, SEND_LEAD)
@@ -444,7 +454,7 @@
     reply = routed_pass(shards, arrived, all_keys, all_values)
     answers = exchange(reply, REPLY_LEAD)
     base, own_out, ours, same, flags = own_pass(
-        near_moves + far_moves, sub_count, shards, route, queries, all_keys, all_values
+        near_moves + far_moves, sub_count, shards, table, queries, all_keys, all_values
     )
     return pl.pallas_call(
         merge_kernel,

time: 34.1 us -> 34.1 us (level)
  Pallas kernels: 10.6 us -> 10.2 us
  waiting for transfers between devices: 6.95 us -> 7.31 us
    all_to_all x2, waiting for transfers between devices: 4.41 us -> 4.75 us  [exchange(): lax.all_to_all(parted, 'ctx', split_axis=0, concat_axis=0, tiled=True, ax...]
    pallas_call x1, Pallas kernels: 5.38 us -> 5.04 us  [own_pass(): pl.pallas_call(functools.partial(own_kernel, moves, sub_count), out_shape...]
  transfers between devices with their start and end apart: 8 -> 8, of which waited for: 3 -> 3; matrix products, arithmetic and copies ran while one was open for 0% -> 0% of each run, Pallas kernels for 22% -> 21%
where the time goes in v4:
time: 34.1 us; the launch traced here: 33.7 us
  starting transfers between devices  16.1 us (47%)
  Pallas kernels  10.2 us (30%)
  waiting for transfers between devices  7.31 us (21%)
    all_to_all x2, starting transfers between devices, exchange(): lax.all_to_all(parted, 'ctx', split_axis=0, concat_axis=0, tiled=True, ax...  12.5 us
    pallas_call x1, Pallas kernels, own_pass(): pl.pallas_call(functools.partial(own_kernel, moves, sub_count), out_shape...  5.04 us
    all_to_all x2, waiting for transfers between devices, exchange(): lax.all_to_all(parted, 'ctx', split_axis=0, concat_axis=0, tiled=True, ax...  4.75 us
    ppermute x2, starting transfers between devices, shift(): lax.ppermute(x, 'sub', [(s, (s + step * CORES) % sub_count) for s in rang...  2.99 us
    pallas_call x1, Pallas kernels, routed_pass(): pl.pallas_call(functools.partial(routed_kernel, count, shards), out_shape...  2.61 us
    ppermute x2, waiting for transfers between devices, shift(): lax.ppermute(x, 'sub', [(s, (s + step * CORES) % sub_count) for s in rang...  2.55 us
    pallas_call x1, Pallas kernels, on_device(): pl.pallas_call(pack_kernel, out_shape=jax.ShapeDtypeStruct((shards * span...  1.88 us
    pallas_call x1, Pallas kernels, on_device(): pl.pallas_call(merge_kernel, out_shape=(jax.ShapeDtypeStruct(own_out.shap...  0.72 us
  transfers between devices with their start and end apart: 8, of which 3 were waited for; matrix products, arithmetic and copies ran while one was open for 0% of the time, Pallas kernels for 21%

profile of v4, /device:TPU:0, one launch (start us, length us, event | category | flops | bytes accessed | tf_op | source)
XLA Modules:
  0.0 33.7 jit_solution(13427769086597750611)
XLA Ops:
  0.0 3.0 %collective-permute-start.1 = (f32[256,256]{1,0:T(8,128)}, f32[256,256]{1,0:T(8,128)S(1)}, u32[]{:S(2)}, u32[]{:S(2)}) collective-permute-start(f32[256,256]{1,0:T(8,128)} %bitcast.9), channel_id=1, source_target_pairs={{0,2},{1,3},{2,0},{3,1},{4,6},{5,7},{6,4},{7,5},{8,10},{9,11},{10,... | collective-permute-start | bytes 786440 | tf_op jit(solution)/shard_map/ppermute | solution.py:418
  3.0 0.0 collective-permute-start.4
  3.0 1.9 %pack.1 = f32[528,128]{1,0:T(8,128)} custom-call(s32[3,2,8]{2,1,0:T(2,128)} %bitcast.17, f32[8,32,512]{2,1,0:T(8,128)} %q_hbm.1), custom_call_target="tpu_custom_call" | custom-call | tf_op jit(solution)/shard_map/pack/pallas_call | solution.py:427
  4.9 0.0 copy-start.1
  4.9 0.0 copy-start.2
  4.9 7.0 %all-to-all-start = ((f32[8,33,2,128]{3,2,1,0:T(2,128)}), f32[8,33,2,128]{3,2,1,0:T(2,128)S(1)}, u32[]{:S(2)}, u32[]{:S(2)}) async-start(f32[8,33,2,128]{3,2,1,0:T(2,128)} %bitcast.3), calls=%async_computation | async-start | bytes 540672 | tf_op jit(solution)/shard_map/all_to_all | solution.py:409
  12.0 0.0 copy-done.1
  12.0 0.0 collective-permute-start
  12.0 0.0 copy-done.2
  12.0 0.5 %collective-permute-start.3 = (f32[256,256]{1,0:T(8,128)S(1)}, f32[256,256]{1,0:T(8,128)S(1)}, u32[]{:S(2)}, u32[]{:S(2)}) collective-permute-start(f32[256,256]{1,0:T(8,128)S(1)} %bitcast.14), channel_id=1, source_target_pairs={{0,1},{1,0},{2,3},{3,2},{4,5},{5,4},{6,7},{7,6},{8,9},{9,8},{10,11... | collective-permute-start | bytes 786440 | tf_op jit(solution)/shard_map/ppermute | solution.py:415
  12.5 0.0 collective-permute-done.1.refs_2_
  12.5 0.1 collective-permute-start.2
  12.6 2.5 %collective-permute-done.4.refs_6_ = f32[256,256]{1,0:T(8,128)S(1)} collective-permute-done((f32[256,256]{1,0:T(8,128)}, f32[256,256]{1,0:T(8,128)S(1)}, u32[]{:S(2)}, u32[]{:S(2)}) %collective-permute-start.4) | collective-permute-done | bytes 262176 | tf_op jit(solution)/shard_map/ppermute | solution.py:418
  15.1 0.0 collective-permute-start.5
  15.1 0.0 collective-permute-done.refs_1_
  15.1 0.0 collective-permute-done.3.refs_5_
  15.1 3.0 %all-to-all-done = f32[8,33,2,128]{3,2,1,0:T(2,128)S(1)} async-done(((f32[8,33,2,128]{3,2,1,0:T(2,128)}), f32[8,33,2,128]{3,2,1,0:T(2,128)S(1)}, u32[]{:S(2)}, u32[]{:S(2)}) %all-to-all-start) | async-done | bytes 270368 | tf_op jit(solution)/shard_map/all_to_all | solution.py:409
  18.1 0.0 collective-permute-done.2.refs_3_
  18.1 0.0 collective-permute-done.5.refs_7_
  18.1 2.6 %routed.1 = f32[528,128]{1,0:T(8,128)} custom-call(f32[528,128]{1,0:T(8,128)S(1)} %bitcast.7, f32[256,256]{1,0:T(8,128)S(1)} %bitcast.11, f32[256,256]{1,0:T(8,128)S(1)} %collective-permute-done.refs_1_, f32[256,256]{1,0:T(8,128)S(1)} %collective-permute-done.1.refs_2_, f32[256,256]{1,0:T(8,128)S(1)} %collective-permute-done.2.refs_3_, ...), custom_call_target="tpu_custom_call" | custom-call | tf_op jit(solution)/shard_map/routed/pallas_call | solution.py:315
  20.7 0.0 copy-start
  20.7 5.5 %all-to-all-start.1 = ((f32[8,33,2,128]{3,2,1,0:T(2,128)}), f32[8,33,2,128]{3,2,1,0:T(2,128)S(1)}, u32[]{:S(2)}, u32[]{:S(2)}) async-start(f32[8,33,2,128]{3,2,1,0:T(2,128)} %bitcast.5), calls=%async_computation.1 | async-start | bytes 540672 | tf_op jit(solution)/shard_map/all_to_all | solution.py:409
  26.2 0.0 copy-done
  26.2 5.0 %own.1 = (f32[8,32,512]{2,1,0:T(8,128)}, f32[8,32,512]{2,1,0:T(8,128)S(1)}, f32[8,128]{1,0:T(8,128)S(1)}, f32[8,8,128]{2,1,0:T(8,128)S(1)}, s32[8]{0:T(128)S(1)}) custom-call(s32[3,2,8]{2,1,0:T(2,128)} %bitcast.18, f32[8,32,512]{2,1,0:T(8,128)S(1)} %copy-done, f32[256,256]{1,0:T(8,128)S(1)} %bitcast.12, f32[256,256]{1,0:T(8,128)S(1)} %collective-permute-done.refs_1_, ...), custom_call_target="tpu_custom_call" | custom-call | tf_op jit(solution)/shard_map/own/pallas_call | solution.py:225
  31.2 1.8 %all-to-all-done.1 = f32[8,33,2,128]{3,2,1,0:T(2,128)S(1)} async-done(((f32[8,33,2,128]{3,2,1,0:T(2,128)}), f32[8,33,2,128]{3,2,1,0:T(2,128)S(1)}, u32[]{:S(2)}, u32[]{:S(2)}) %all-to-all-start.1) | async-done | bytes 270368 | tf_op jit(solution)/shard_map/all_to_all | solution.py:409
  33.0 0.7 %merge.1 = (f32[8,32,512]{2,1,0:T(8,128)S(1)}, f32[8,32,512]{2,1,0:T(8,128)}) custom-call(s32[8]{0:T(128)S(1)} %get-tuple-element.11.flag_vmem, f32[528,128]{1,0:T(8,128)S(1)} %bitcast.8, f32[8,128]{1,0:T(8,128)S(1)} %get-tuple-element.12.ours_ref, f32[8,8,128]{2,1,0:T(8,128)S(1)} %get-tuple-element.13.same_ref, ...), custom_call_target="tpu_custom_call", output_to_operand_aliasing={{0}: (4, {}), {1}: (5, {})} | custom-call | tf_op jit(solution)/shard_map/merge/pallas_call | solution.py:459
Async XLA Ops:
  0.0 12.5 %collective-permute-start.1 = (f32[256,256]{1,0:T(8,128)}, f32[256,256]{1,0:T(8,128)S(1)}, u32[]{:S(2)}, u32[]{:S(2)}) collective-permute-start(f32[256,256]{1,0:T(8,128)} %bitcast.9), channel_id=1, source_target_pairs={{0,2},{1,3},{2,0},{3,1},{4,6},{5,7},{6,4},{7,5},{8,10},{9,11},{10,... | collective-permute-start | bytes 786440 | tf_op jit(solution)/shard_map/ppermute | solution.py:418
  3.0 12.1 %collective-permute-start.4 = (f32[256,256]{1,0:T(8,128)}, f32[256,256]{1,0:T(8,128)S(1)}, u32[]{:S(2)}, u32[]{:S(2)}) collective-permute-start(f32[256,256]{1,0:T(8,128)} %bitcast.13), channel_id=1, source_target_pairs={{0,2},{1,3},{2,0},{3,1},{4,6},{5,7},{6,4},{7,5},{8,10},{9,11},{10,... | collective-permute-start | bytes 786440 | tf_op jit(solution)/shard_map/ppermute | solution.py:418
  4.9 7.1 %copy-start.1 = (f32[1,256,256]{2,1,0:T(8,128)S(1)}, f32[1,256,256]{2,1,0:T(8,128)}, u32[]{:S(2)}) copy-start(f32[1,256,256]{2,1,0:T(8,128)} %param.5) | copy-start | bytes 786436
  4.9 7.1 %copy-start.2 = (f32[1,256,256]{2,1,0:T(8,128)S(1)}, f32[1,256,256]{2,1,0:T(8,128)}, u32[]{:S(2)}) copy-start(f32[1,256,256]{2,1,0:T(8,128)} %param.6) | copy-start | bytes 786436
  4.9 13.2 %all-to-all-start = ((f32[8,33,2,128]{3,2,1,0:T(2,128)}), f32[8,33,2,128]{3,2,1,0:T(2,128)S(1)}, u32[]{:S(2)}, u32[]{:S(2)}) async-start(f32[8,33,2,128]{3,2,1,0:T(2,128)} %bitcast.3), calls=%async_computation | async-start | bytes 540672 | tf_op jit(solution)/shard_map/all_to_all | solution.py:409
  12.0 3.1 %collective-permute-start = (f32[256,256]{1,0:T(8,128)S(1)}, f32[256,256]{1,0:T(8,128)S(1)}, u32[]{:S(2)}, u32[]{:S(2)}) collective-permute-start(f32[256,256]{1,0:T(8,128)S(1)} %bitcast.10), channel_id=1, source_target_pairs={{0,1},{1,0},{2,3},{3,2},{4,5},{5,4},{6,7},{7,6},{8,9},{9,8},{10,11... | collective-permute-start | bytes 786440 | tf_op jit(solution)/shard_map/ppermute | solution.py:415
  12.0 3.1 %collective-permute-start.3 = (f32[256,256]{1,0:T(8,128)S(1)}, f32[256,256]{1,0:T(8,128)S(1)}, u32[]{:S(2)}, u32[]{:S(2)}) collective-permute-start(f32[256,256]{1,0:T(8,128)S(1)} %bitcast.14), channel_id=1, source_target_pairs={{0,1},{1,0},{2,3},{3,2},{4,5},{5,4},{6,7},{7,6},{8,9},{9,8},{10,11... | collective-permute-start | bytes 786440 | tf_op jit(solution)/shard_map/ppermute | solution.py:415
  12.5 5.6 %collective-permute-start.2 = (f32[256,256]{1,0:T(8,128)S(1)}, f32[256,256]{1,0:T(8,128)S(1)}, u32[]{:S(2)}, u32[]{:S(2)}) collective-permute-start(f32[256,256]{1,0:T(8,128)S(1)} %collective-permute-done.1.refs_2_), channel_id=1, source_target_pairs={{0,1},{1,0},{2,3},{3,2},{4,5},{5,4},{6,7},{7,6},{8,9},{9,8},{10,11... | collective-permute-start | bytes 786440 | tf_op jit(solution)/shard_map/ppermute | solution.py:415
  15.1 3.0 %collective-permute-start.5 = (f32[256,256]{1,0:T(8,128)S(1)}, f32[256,256]{1,0:T(8,128)S(1)}, u32[]{:S(2)}, u32[]{:S(2)}) collective-permute-start(f32[256,256]{1,0:T(8,128)S(1)} %collective-permute-done.4.refs_6_), channel_id=1, source_target_pairs={{0,1},{1,0},{2,3},{3,2},{4,5},{5,4},{6,7},{7,6},{8,9},{9,8},{10,11... | collective-permute-start | bytes 786440 | tf_op jit(solution)/shard_map/ppermute | solution.py:415
  20.7 5.5 %copy-start = (f32[8,32,512]{2,1,0:T(8,128)S(1)}, f32[8,32,512]{2,1,0:T(8,128)}, u32[]{:S(2)}) copy-start(f32[8,32,512]{2,1,0:T(8,128)} %q_hbm.1) | copy-start | bytes 1572868
  20.7 12.3 %all-to-all-start.1 = ((f32[8,33,2,128]{3,2,1,0:T(2,128)}), f32[8,33,2,128]{3,2,1,0:T(2,128)S(1)}, u32[]{:S(2)}, u32[]{:S(2)}) async-start(f32[8,33,2,128]{3,2,1,0:T(2,128)} %bitcast.5), calls=%async_computation.1 | async-start | bytes 540672 | tf_op jit(solution)/shard_map/all_to_all | solution.py:409

commit v5 on v4

--- a/solution.py
+++ b/solution.py
@@ -424,7 +424,7 @@
     near_keys, near_values = [keys, swap(keys)], [values, swap(values)]
 
     table = pltpu.with_memory_space_constraint(jnp.transpose(selected, (2, 1, 0)), pltpu.HBM)
-    packed = pl.pallas_call(
+    pack = pl.pallas_call(
         pack_kernel,
         out_shape=jax.ShapeDtypeStruct((shards * span, LANES), jnp.float32),
         in_specs=[HBM, HBM],
@@ -438,10 +438,8 @@
         ],
         compiler_params=PARAMS,
         name="pack",
-    )(
-        table,
-        pltpu.with_memory_space_constraint(queries, pltpu.HBM),
-    )
+    )
+    packed = pack(table, pltpu.with_memory_space_constraint(queries, pltpu.HBM))
     arrived = exchange(packed, SEND_LEAD)
 
     near_moves = ((0, False), (0, True))

time: 34.1 us -> 34.1 us (level)
  no operation moved by 1% of the time
where the time goes in v5:
time: 34.1 us; the launch traced here: 33.7 us
  starting transfers between devices  16.1 us (47%)
  Pallas kernels  10.2 us (30%)
  waiting for transfers between devices  7.31 us (21%)
    all_to_all x2, starting transfers between devices, exchange(): lax.all_to_all(parted, 'ctx', split_axis=0, concat_axis=0, tiled=True, ax...  12.5 us
    pallas_call x1, Pallas kernels, own_pass(): pl.pallas_call(functools.partial(own_kernel, moves, sub_count), out_shape...  5.04 us
    all_to_all x2, waiting for transfers between devices, exchange(): lax.all_to_all(parted, 'ctx', split_axis=0, concat_axis=0, tiled=True, ax...  4.75 us
    ppermute x2, starting transfers between devices, shift(): lax.ppermute(x, 'sub', [(s, (s + step * CORES) % sub_count) for s in rang...  2.99 us
    pallas_call x1, Pallas kernels, routed_pass(): pl.pallas_call(functools.partial(routed_kernel, count, shards), out_shape...  2.61 us
    ppermute x2, waiting for transfers between devices, shift(): lax.ppermute(x, 'sub', [(s, (s + step * CORES) % sub_count) for s in rang...  2.55 us
    pallas_call x1, Pallas kernels, on_device(): packed = pack(table, pltpu.with_memory_space_constraint(queries, pltpu.HBM))  1.88 us
    pallas_call x1, Pallas kernels, on_device(): pl.pallas_call(merge_kernel, out_shape=(jax.ShapeDtypeStruct(own_out.shap...  0.72 us
  transfers between devices with their start and end apart: 8, of which 3 were waited for; matrix products, arithmetic and copies ran while one was open for 0% of the time, Pallas kernels for 21%

profile of v5, /device:TPU:0, one launch (start us, length us, event | category | flops | bytes accessed | tf_op | source)
XLA Modules:
  0.0 33.7 jit_solution(13427769086597750611)
XLA Ops:
  0.0 3.0 %collective-permute-start.1 = (f32[256,256]{1,0:T(8,128)}, f32[256,256]{1,0:T(8,128)S(1)}, u32[]{:S(2)}, u32[]{:S(2)}) collective-permute-start(f32[256,256]{1,0:T(8,128)} %bitcast.9), channel_id=1, source_target_pairs={{0,2},{1,3},{2,0},{3,1},{4,6},{5,7},{6,4},{7,5},{8,10},{9,11},{10,... | collective-permute-start | bytes 786440 | tf_op jit(solution)/shard_map/ppermute | solution.py:418
  3.0 0.0 collective-permute-start.4
  3.0 1.9 %pack.1 = f32[528,128]{1,0:T(8,128)} custom-call(s32[3,2,8]{2,1,0:T(2,128)} %bitcast.17, f32[8,32,512]{2,1,0:T(8,128)} %q_hbm.1), custom_call_target="tpu_custom_call" | custom-call | tf_op jit(solution)/shard_map/pack/pallas_call | solution.py:442
  4.9 0.0 copy-start.1
  4.9 0.0 copy-start.2
  4.9 7.0 %all-to-all-start = ((f32[8,33,2,128]{3,2,1,0:T(2,128)}), f32[8,33,2,128]{3,2,1,0:T(2,128)S(1)}, u32[]{:S(2)}, u32[]{:S(2)}) async-start(f32[8,33,2,128]{3,2,1,0:T(2,128)} %bitcast.3), calls=%async_computation | async-start | bytes 540672 | tf_op jit(solution)/shard_map/all_to_all | solution.py:409
  12.0 0.0 copy-done.1
  12.0 0.0 collective-permute-start
  12.0 0.0 copy-done.2
  12.0 0.5 %collective-permute-start.3 = (f32[256,256]{1,0:T(8,128)S(1)}, f32[256,256]{1,0:T(8,128)S(1)}, u32[]{:S(2)}, u32[]{:S(2)}) collective-permute-start(f32[256,256]{1,0:T(8,128)S(1)} %bitcast.14), channel_id=1, source_target_pairs={{0,1},{1,0},{2,3},{3,2},{4,5},{5,4},{6,7},{7,6},{8,9},{9,8},{10,11... | collective-permute-start | bytes 786440 | tf_op jit(solution)/shard_map/ppermute | solution.py:415
  12.5 0.0 collective-permute-done.1.refs_2_
  12.5 0.1 collective-permute-start.2
  12.6 2.5 %collective-permute-done.4.refs_6_ = f32[256,256]{1,0:T(8,128)S(1)} collective-permute-done((f32[256,256]{1,0:T(8,128)}, f32[256,256]{1,0:T(8,128)S(1)}, u32[]{:S(2)}, u32[]{:S(2)}) %collective-permute-start.4) | collective-permute-done | bytes 262176 | tf_op jit(solution)/shard_map/ppermute | solution.py:418
  15.1 0.0 collective-permute-start.5
  15.1 0.0 collective-permute-done.refs_1_
  15.1 0.0 collective-permute-done.3.refs_5_
  15.1 3.0 %all-to-all-done = f32[8,33,2,128]{3,2,1,0:T(2,128)S(1)} async-done(((f32[8,33,2,128]{3,2,1,0:T(2,128)}), f32[8,33,2,128]{3,2,1,0:T(2,128)S(1)}, u32[]{:S(2)}, u32[]{:S(2)}) %all-to-all-start) | async-done | bytes 270368 | tf_op jit(solution)/shard_map/all_to_all | solution.py:409
  18.1 0.0 collective-permute-done.2.refs_3_
  18.1 0.0 collective-permute-done.5.refs_7_
  18.1 2.6 %routed.1 = f32[528,128]{1,0:T(8,128)} custom-call(f32[528,128]{1,0:T(8,128)S(1)} %bitcast.7, f32[256,256]{1,0:T(8,128)S(1)} %bitcast.11, f32[256,256]{1,0:T(8,128)S(1)} %collective-permute-done.refs_1_, f32[256,256]{1,0:T(8,128)S(1)} %collective-permute-done.1.refs_2_, f32[256,256]{1,0:T(8,128)S(1)} %collective-permute-done.2.refs_3_, ...), custom_call_target="tpu_custom_call" | custom-call | tf_op jit(solution)/shard_map/routed/pallas_call | solution.py:315
  20.7 0.0 copy-start
  20.7 5.5 %all-to-all-start.1 = ((f32[8,33,2,128]{3,2,1,0:T(2,128)}), f32[8,33,2,128]{3,2,1,0:T(2,128)S(1)}, u32[]{:S(2)}, u32[]{:S(2)}) async-start(f32[8,33,2,128]{3,2,1,0:T(2,128)} %bitcast.5), calls=%async_computation.1 | async-start | bytes 540672 | tf_op jit(solution)/shard_map/all_to_all | solution.py:409
  26.2 0.0 copy-done
  26.2 5.0 %own.1 = (f32[8,32,512]{2,1,0:T(8,128)}, f32[8,32,512]{2,1,0:T(8,128)S(1)}, f32[8,128]{1,0:T(8,128)S(1)}, f32[8,8,128]{2,1,0:T(8,128)S(1)}, s32[8]{0:T(128)S(1)}) custom-call(s32[3,2,8]{2,1,0:T(2,128)} %bitcast.18, f32[8,32,512]{2,1,0:T(8,128)S(1)} %copy-done, f32[256,256]{1,0:T(8,128)S(1)} %bitcast.12, f32[256,256]{1,0:T(8,128)S(1)} %collective-permute-done.refs_1_, ...), custom_call_target="tpu_custom_call" | custom-call | tf_op jit(solution)/shard_map/own/pallas_call | solution.py:225
  31.2 1.8 %all-to-all-done.1 = f32[8,33,2,128]{3,2,1,0:T(2,128)S(1)} async-done(((f32[8,33,2,128]{3,2,1,0:T(2,128)}), f32[8,33,2,128]{3,2,1,0:T(2,128)S(1)}, u32[]{:S(2)}, u32[]{:S(2)}) %all-to-all-start.1) | async-done | bytes 270368 | tf_op jit(solution)/shard_map/all_to_all | solution.py:409
  33.0 0.7 %merge.1 = (f32[8,32,512]{2,1,0:T(8,128)S(1)}, f32[8,32,512]{2,1,0:T(8,128)}) custom-call(s32[8]{0:T(128)S(1)} %get-tuple-element.11.flag_vmem, f32[528,128]{1,0:T(8,128)S(1)} %bitcast.8, f32[8,128]{1,0:T(8,128)S(1)} %get-tuple-element.12.ours_ref, f32[8,8,128]{2,1,0:T(8,128)S(1)} %get-tuple-element.13.same_ref, ...), custom_call_target="tpu_custom_call", output_to_operand_aliasing={{0}: (4, {}), {1}: (5, {})} | custom-call | tf_op jit(solution)/shard_map/merge/pallas_call | solution.py:457
Async XLA Ops:
  0.0 12.5 %collective-permute-start.1 = (f32[256,256]{1,0:T(8,128)}, f32[256,256]{1,0:T(8,128)S(1)}, u32[]{:S(2)}, u32[]{:S(2)}) collective-permute-start(f32[256,256]{1,0:T(8,128)} %bitcast.9), channel_id=1, source_target_pairs={{0,2},{1,3},{2,0},{3,1},{4,6},{5,7},{6,4},{7,5},{8,10},{9,11},{10,... | collective-permute-start | bytes 786440 | tf_op jit(solution)/shard_map/ppermute | solution.py:418
  3.0 12.1 %collective-permute-start.4 = (f32[256,256]{1,0:T(8,128)}, f32[256,256]{1,0:T(8,128)S(1)}, u32[]{:S(2)}, u32[]{:S(2)}) collective-permute-start(f32[256,256]{1,0:T(8,128)} %bitcast.13), channel_id=1, source_target_pairs={{0,2},{1,3},{2,0},{3,1},{4,6},{5,7},{6,4},{7,5},{8,10},{9,11},{10,... | collective-permute-start | bytes 786440 | tf_op jit(solution)/shard_map/ppermute | solution.py:418
  4.9 7.1 %copy-start.1 = (f32[1,256,256]{2,1,0:T(8,128)S(1)}, f32[1,256,256]{2,1,0:T(8,128)}, u32[]{:S(2)}) copy-start(f32[1,256,256]{2,1,0:T(8,128)} %param.5) | copy-start | bytes 786436
  4.9 7.1 %copy-start.2 = (f32[1,256,256]{2,1,0:T(8,128)S(1)}, f32[1,256,256]{2,1,0:T(8,128)}, u32[]{:S(2)}) copy-start(f32[1,256,256]{2,1,0:T(8,128)} %param.6) | copy-start | bytes 786436
  4.9 13.2 %all-to-all-start = ((f32[8,33,2,128]{3,2,1,0:T(2,128)}), f32[8,33,2,128]{3,2,1,0:T(2,128)S(1)}, u32[]{:S(2)}, u32[]{:S(2)}) async-start(f32[8,33,2,128]{3,2,1,0:T(2,128)} %bitcast.3), calls=%async_computation | async-start | bytes 540672 | tf_op jit(solution)/shard_map/all_to_all | solution.py:409
  12.0 3.1 %collective-permute-start = (f32[256,256]{1,0:T(8,128)S(1)}, f32[256,256]{1,0:T(8,128)S(1)}, u32[]{:S(2)}, u32[]{:S(2)}) collective-permute-start(f32[256,256]{1,0:T(8,128)S(1)} %bitcast.10), channel_id=1, source_target_pairs={{0,1},{1,0},{2,3},{3,2},{4,5},{5,4},{6,7},{7,6},{8,9},{9,8},{10,11... | collective-permute-start | bytes 786440 | tf_op jit(solution)/shard_map/ppermute | solution.py:415
  12.0 3.1 %collective-permute-start.3 = (f32[256,256]{1,0:T(8,128)S(1)}, f32[256,256]{1,0:T(8,128)S(1)}, u32[]{:S(2)}, u32[]{:S(2)}) collective-permute-start(f32[256,256]{1,0:T(8,128)S(1)} %bitcast.14), channel_id=1, source_target_pairs={{0,1},{1,0},{2,3},{3,2},{4,5},{5,4},{6,7},{7,6},{8,9},{9,8},{10,11... | collective-permute-start | bytes 786440 | tf_op jit(solution)/shard_map/ppermute | solution.py:415
  12.5 5.6 %collective-permute-start.2 = (f32[256,256]{1,0:T(8,128)S(1)}, f32[256,256]{1,0:T(8,128)S(1)}, u32[]{:S(2)}, u32[]{:S(2)}) collective-permute-start(f32[256,256]{1,0:T(8,128)S(1)} %collective-permute-done.1.refs_2_), channel_id=1, source_target_pairs={{0,1},{1,0},{2,3},{3,2},{4,5},{5,4},{6,7},{7,6},{8,9},{9,8},{10,11... | collective-permute-start | bytes 786440 | tf_op jit(solution)/shard_map/ppermute | solution.py:415
  15.1 3.0 %collective-permute-start.5 = (f32[256,256]{1,0:T(8,128)S(1)}, f32[256,256]{1,0:T(8,128)S(1)}, u32[]{:S(2)}, u32[]{:S(2)}) collective-permute-start(f32[256,256]{1,0:T(8,128)S(1)} %collective-permute-done.4.refs_6_), channel_id=1, source_target_pairs={{0,1},{1,0},{2,3},{3,2},{4,5},{5,4},{6,7},{7,6},{8,9},{9,8},{10,11... | collective-permute-start | bytes 786440 | tf_op jit(solution)/shard_map/ppermute | solution.py:415
  20.7 5.5 %copy-start = (f32[8,32,512]{2,1,0:T(8,128)S(1)}, f32[8,32,512]{2,1,0:T(8,128)}, u32[]{:S(2)}) copy-start(f32[8,32,512]{2,1,0:T(8,128)} %q_hbm.1) | copy-start | bytes 1572868
  20.7 12.3 %all-to-all-start.1 = ((f32[8,33,2,128]{3,2,1,0:T(2,128)}), f32[8,33,2,128]{3,2,1,0:T(2,128)S(1)}, u32[]{:S(2)}, u32[]{:S(2)}) async-start(f32[8,33,2,128]{3,2,1,0:T(2,128)} %bitcast.5), calls=%async_computation.1 | async-start | bytes 540672 | tf_op jit(solution)/shard_map/all_to_all | solution.py:409
